TPU v7x, 512 devices: a whole 4x4x16 slice. The times are simulated.
512 devices in a mesh: section: 8 (over x, y_hi), fsdp: 64 (over z, y_lo, core).
Axes of the slice: x: 4, y: 4 (y_hi: 2, y_lo: 2; y = y_hi * 2 + y_lo), z: 16, core: 2. Of those that a mesh axis runs over, the one named last changes fastest.
Arguments:
- tokens: bfloat16 [6, 2048, 4096], P(None, 'fsdp'), may hold values from -16 to 16
- cotangent: bfloat16 [6, 2048, 4096], P(None, 'fsdp'), may hold values from -16 to 16
- order: int32 [6], replicated, may hold values from 0 to 5, each once
- w_value: bfloat16 [8, 4096, 512], P('section', 'fsdp'), may hold values from -0.09375 to 0.09375
- w_out: bfloat16 [8, 512, 4096], P('section', None, 'fsdp'), may hold values from -0.25 to 0.25
- adapter_down: bfloat16 [8, 4096, 128], P('section', 'fsdp'), may hold values from -0.09375 to 0.09375
- adapter_up: bfloat16 [8, 128, 512], P('section', None, 'fsdp'), may hold values from -0.5 to 0.5
Outputs:
- input_grads: bfloat16 [8, 6, 2048, 4096], P('section', None, 'fsdp')
- grad_down: float32 [8, 4096, 128], P('section', 'fsdp')
- grad_up: float32 [8, 128, 512], P('section', None, 'fsdp')
Inputs may be any that keep to these rules, and one draw needn't show every extreme that they name: order names each microbatch 0 .. 5 exactly once.
All inputs are finite; a program needn't handle non-finite values.
Results may differ from a plain program's by a relative error of at most 0.02.
Values may be sent and summed in bfloat16 or wider, within the bound.
A program may use at most 128 MiB of HBM per device.

v0:
```python
import jax
import jax.numpy as jnp
from jax import lax
from jax.sharding import PartitionSpec as P

epsilon = 1e-05


def joined_along(pieces, dim):
    pieces = jnp.moveaxis(pieces, 0, dim)
    lengths = pieces.shape
    return pieces.reshape(*lengths[:dim], lengths[dim] * lengths[dim + 1], *lengths[dim + 2 :])


def gather_packed(arrays, axis, dims):
    ravelled = jnp.concatenate([a.reshape(-1) for a in arrays])
    lines, at, gathered = (lax.all_gather(ravelled, axis), 0, [])
    for a, dim in zip(arrays, dims):
        pieces = lines[:, at : at + a.size].reshape(-1, *a.shape)
        gathered.append(joined_along(pieces, dim))
        at += a.size
    return tuple(gathered)


def from_behind(block, axis, distance):
    devices = range(lax.axis_size(axis))
    route = [(i - distance, i) for i in devices if i - distance in devices]
    return lax.ppermute(block, axis, route)


def split_up(value, dim, devices):
    lengths = value.shape
    pieces = value.reshape(*lengths[:dim], devices, lengths[dim] // devices, *lengths[dim + 1 :])
    return jnp.moveaxis(pieces, dim, 0)


def sum_at_owner(value, axis, dim):
    devices = lax.axis_size(axis)
    pieces = lax.all_to_all(split_up(value, dim, devices), axis, 0, 0, tiled=True)
    return jnp.sum(pieces.astype(jnp.float32), axis=0)


def layer_forward(inputs, w_val, w_proj, a_down, a_up):
    widened = inputs.astype(jnp.float32)
    inverse = lax.rsqrt(jnp.mean(widened * widened, axis=-1, keepdims=True) + epsilon)
    normed = (widened * inverse).astype(jnp.bfloat16)
    low = jnp.dot(normed, a_down, preferred_element_type=jnp.float32).astype(jnp.bfloat16)
    values = (
        jnp.dot(normed, w_val, preferred_element_type=jnp.float32)
        + jnp.dot(low, a_up, preferred_element_type=jnp.float32)
    ).astype(jnp.bfloat16)
    outputs = (widened + jnp.dot(values, w_proj, preferred_element_type=jnp.float32)).astype(
        jnp.bfloat16
    )
    return (outputs, normed, low, inverse)


def layer_backward(inputs, inverse, upstream, w_val, w_proj, a_down, a_up):
    d_values = jnp.dot(upstream, w_proj.T, preferred_element_type=jnp.float32).astype(jnp.bfloat16)
    d_low = jnp.dot(d_values, a_up.T, preferred_element_type=jnp.float32).astype(jnp.bfloat16)
    d_normed = jnp.dot(d_values, w_val.T, preferred_element_type=jnp.float32) + jnp.dot(
        d_low, a_down.T, preferred_element_type=jnp.float32
    )
    widened = inputs.astype(jnp.float32)
    project = jnp.mean(d_normed * widened, axis=-1, keepdims=True)
    d_inputs = upstream.astype(jnp.float32) + inverse * (
        d_normed - widened * inverse * inverse * project
    )
    return (d_inputs.astype(jnp.bfloat16), d_values, d_low)


def store(buffer, item, clipped, in_range):
    previous = lax.dynamic_index_in_dim(buffer, clipped, 0, keepdims=False)
    return lax.dynamic_update_index_in_dim(buffer, jnp.where(in_range, item, previous), clipped, 0)


def contract_rows(left, right):
    return lax.dot_general(
        left, right, (((0,), (0,)), ((), ())), preferred_element_type=jnp.float32
    )


def body(tokens, cotangent, order, w_value, w_out, adapter_down, adapter_up):
    sections = lax.axis_size("section")
    position = lax.axis_index("section")
    count_micro = tokens.shape[0]
    local_tokens = tokens.shape[1]
    features = tokens.shape[2]
    rank = adapter_down.shape[2]
    gathered = gather_packed((w_value, w_out, adapter_down, adapter_up), "fsdp", (1, 2, 1, 2))
    full_val = gathered[0][0]
    full_proj = gathered[1][0]
    full_down = gathered[2][0]
    full_up = gathered[3][0]
    value_width = full_val.shape[1]
    moments = jnp.arange(count_micro + sections - 1, dtype=jnp.int32)

    def run_forward(inputs):
        return layer_forward(inputs, full_val, full_proj, full_down, full_up)

    def skip_forward(inputs):
        return (
            jnp.zeros((local_tokens, features), jnp.bfloat16),
            jnp.zeros((local_tokens, features), jnp.bfloat16),
            jnp.zeros((local_tokens, rank), jnp.bfloat16),
            jnp.zeros((local_tokens, 1), jnp.float32),
        )

    def forward_step(carry, moment):
        incoming, keep_in, keep_norm, keep_low, keep_inv = carry
        index_slot = moment - position
        in_range = (index_slot >= 0) & (index_slot < count_micro)
        clipped = jnp.clip(index_slot, 0, count_micro - 1)
        entering = tokens[order[clipped]]
        inputs = jnp.where(position == 0, entering, incoming)
        outputs, normed, low, inverse = lax.cond(in_range, run_forward, skip_forward, inputs)
        keep_in = store(keep_in, inputs, clipped, in_range)
        keep_norm = store(keep_norm, normed, clipped, in_range)
        keep_low = store(keep_low, low, clipped, in_range)
        keep_inv = store(keep_inv, inverse, clipped, in_range)
        passed = from_behind(outputs, "section", 1)
        return ((passed, keep_in, keep_norm, keep_low, keep_inv), None)

    start_fwd = (
        jnp.zeros((local_tokens, features), jnp.bfloat16),
        jnp.zeros(tokens.shape, jnp.bfloat16),
        jnp.zeros(tokens.shape, jnp.bfloat16),
        jnp.zeros((count_micro, local_tokens, rank), jnp.bfloat16),
        jnp.zeros((count_micro, local_tokens, 1), jnp.float32),
    )
    carried, unused = lax.scan(forward_step, start_fwd, moments)
    saved_in, saved_norm, saved_low, saved_inv = (carried[1], carried[2], carried[3], carried[4])

    def run_backward(operands):
        inputs, inverse, upstream = operands
        return layer_backward(inputs, inverse, upstream, full_val, full_proj, full_down, full_up)

    def skip_backward(operands):
        return (
            jnp.zeros((local_tokens, features), jnp.bfloat16),
            jnp.zeros((local_tokens, value_width), jnp.bfloat16),
            jnp.zeros((local_tokens, rank), jnp.bfloat16),
        )

    def backward_step(carry, moment):
        incoming, keep_dv, keep_dlow, keep_dx = carry
        index_slot = moment - (sections - 1 - position)
        in_range = (index_slot >= 0) & (index_slot < count_micro)
        clipped = jnp.clip(index_slot, 0, count_micro - 1)
        entering = cotangent[order[clipped]]
        upstream = jnp.where(position == sections - 1, entering, incoming)
        inputs = lax.dynamic_index_in_dim(saved_in, clipped, 0, keepdims=False)
        inverse = lax.dynamic_index_in_dim(saved_inv, clipped, 0, keepdims=False)
        d_inputs, d_values, d_low = lax.cond(
            in_range, run_backward, skip_backward, (inputs, inverse, upstream)
        )
        keep_dv = store(keep_dv, d_values, clipped, in_range)
        keep_dlow = store(keep_dlow, d_low, clipped, in_range)
        keep_dx = store(keep_dx, d_inputs, clipped, in_range)
        passed = from_behind(d_inputs, "section", -1)
        return ((passed, keep_dv, keep_dlow, keep_dx), None)

    start_bwd = (
        jnp.zeros((local_tokens, features), jnp.bfloat16),
        jnp.zeros((count_micro, local_tokens, value_width), jnp.bfloat16),
        jnp.zeros((count_micro, local_tokens, rank), jnp.bfloat16),
        jnp.zeros(tokens.shape, jnp.bfloat16),
    )
    carried_back, unused_back = lax.scan(backward_step, start_bwd, moments)
    saved_dv, saved_dlow, saved_dx = (carried_back[1], carried_back[2], carried_back[3])
    normed_flat = saved_norm.reshape(-1, features)
    low_flat = saved_low.reshape(-1, rank)
    dv_flat = saved_dv.reshape(-1, value_width)
    dlow_flat = saved_dlow.reshape(-1, rank)
    share_down = features // lax.axis_size("fsdp")
    share_up = value_width // lax.axis_size("fsdp")
    block_rows = share_down + share_up
    blocks = block_rows * lax.axis_size("fsdp") // block_rows
    part_down = contract_rows(normed_flat, dlow_flat).reshape(blocks, share_down, rank)
    part_up = contract_rows(dv_flat, low_flat).reshape(blocks, share_up, rank)
    combined = sum_at_owner(
        jnp.concatenate([part_down, part_up], axis=1)
        .reshape(block_rows * lax.axis_size("fsdp"), rank)
        .astype(jnp.bfloat16),
        "fsdp",
        0,
    )
    grad_down = combined[:share_down]
    grad_up_rows = combined[share_down:]
    return (saved_dx[None], grad_down[None], grad_up_rows.T[None])


def solution(mesh):
    return jax.shard_map(
        body,
        mesh=mesh,
        in_specs=(
            P(None, "fsdp", None),
            P(None, "fsdp", None),
            P(),
            P("section", "fsdp", None),
            P("section", None, "fsdp"),
            P("section", "fsdp", None),
            P("section", None, "fsdp"),
        ),
        out_specs=(
            P("section", None, "fsdp", None),
            P("section", "fsdp", None),
            P("section", None, "fsdp"),
        ),
        check_vma=False,
    )
```

profile of v0, /device:TPU:25, one launch (start us, length us, event | category | flops | bytes accessed | tf_op | source)
XLA Modules:
  0.0 865.4 jit_solution(3900057460629835657)
XLA Ops:
  11.5 134.1 %all-gather.3.cloned.1.call-done = bf16[4784128]{0:T(1024)(128)(2,1)} async-done(((bf16[74752]{0:T(1024)(128)(2,1)}), bf16[4784128]{0:T(1024)(128)(2,1)}) %all-gather.3.cloned.1.call-update) | async-done | bytes 9568272 | tf_op jit(solution)/shard_map/all_gather | solution.py:17
  145.6 11.3 %reshape.83 = bf16[64,74752]{1,0:T(8,128)(2,1)} reshape(bf16[4784128]{0:T(1024)(128)(2,1)} %all-gather.3.cloned.1.call-done) | data formatting | bytes 19136512 | tf_op jit(solution)/shard_map/all_gather | solution.py:17
  156.9 5.8 fusion.17
  164.4 7.4 squeeze_reshape_transpose_reshape.6
  171.8 11.4 %reshape.77 = bf16[64,1,512,64]{3,2,0,1:T(8,128)(2,1)} reshape(bf16[64,32768]{1,0:T(8,128)(2,1)} %get-tuple-element.592) | data formatting | bytes 8388608 | tf_op jit(solution)/shard_map/reshape | solution.py:19
  183.2 8.6 copy.29
  191.7 6.4 copy.31
  200.3 266.1 %while.37 = (s32[]{:T(128)}, bf16[32,4096]{1,0:T(8,128)(2,1)S(1)}, bf16[6,32,4096]{2,1,0:T(8,128)(2,1)S(1)}, bf16[6,32,4096]{2,1,0:T(8,128)(2,1)}, bf16[6,32,128...) while((s32[]{:T(128)}, bf16[32,4096]{1,0:T(8,128)(2,1)S(1)}, ...), condition=%wide.region_4.5_spmd, body=%wide.region_0.4_spmd.sunk | while | flops 307798080 | bytes 17886068 | solution.py:131
  213.4 8.7 %collective-permute-done = bf16[32,4096]{1,0:T(8,128)(2,1)S(1)} collective-permute-done((bf16[32,4096]{1,0:T(8,128)(2,1)}, bf16[32,4096]{1,0:T(8,128)(2,1)S(1)}, u32[]{:S(2)}, u32[]{:S(2)}) %collective-permute-start) | collective-permute-done | bytes 262176 | tf_op jit(solution)/shard_map/while/body/eval_jaxpr/ppermute | solution.py:28
  227.0 8.2 conditional.4
  231.3 3.9 fusion
  240.9 4.9 collective-permute-done
  250.7 8.2 conditional.4
  255.1 3.9 fusion
  273.6 8.2 conditional.4
  281.8 4.3 collective-permute-start
  295.5 8.2 conditional.4
  303.7 5.5 collective-permute-start
  317.9 8.2 conditional.4
  322.2 3.9 fusion
  326.1 5.9 collective-permute-start
  340.8 8.2 conditional.4
  345.1 3.9 fusion
  349.0 5.9 collective-permute-start
  364.9 12.8 %collective-permute-start = (bf16[32,4096]{1,0:T(8,128)(2,1)}, bf16[32,4096]{1,0:T(8,128)(2,1)S(1)}, u32[]{:S(2)}, u32[]{:S(2)}) collective-permute-start(bf16[32,4096]{1,0:T(8,128)(2,1)} %get-tuple-element.776), channel_id=1, source_target_pairs={{0,64},{64,128},{128,192},{192,256},{256,320},{320,384},{384,448},... | collective-permute-start | bytes 786440 | tf_op jit(solution)/shard_map/while/body/eval_jaxpr/ppermute | solution.py:28
  387.6 6.1 collective-permute-start
  403.6 7.9 collective-permute-start
  421.3 6.1 collective-permute-start
  437.3 9.6 %collective-permute-start = (bf16[32,4096]{1,0:T(8,128)(2,1)}, bf16[32,4096]{1,0:T(8,128)(2,1)S(1)}, u32[]{:S(2)}, u32[]{:S(2)}) collective-permute-start(bf16[32,4096]{1,0:T(8,128)(2,1)} %get-tuple-element.776), channel_id=1, source_target_pairs={{0,64},{64,128},{128,192},{192,256},{256,320},{320,384},{384,448},... | collective-permute-start | bytes 786440 | tf_op jit(solution)/shard_map/while/body/eval_jaxpr/ppermute | solution.py:28
  456.8 6.1 collective-permute-start
  468.5 291.6 %while.38 = (s32[]{:T(128)}, bf16[32,4096]{1,0:T(8,128)(2,1)S(1)}, bf16[6,32,512]{2,1,0:T(8,128)(2,1)S(1)}, bf16[6,32,128]{2,1,0:T(8,128)(2,1)}, bf16[6,32,4096]...) while((s32[]{:T(128)}, bf16[32,4096]{1,0:T(8,128)(2,1)S(1)}, ...), condition=%wide.region_9.10_spmd, body=%wide.region_5.9_spmd.sunk | while | flops 308322304 | bytes 33221568 | solution.py:169
  475.4 6.6 collective-permute-done.1
  488.9 7.8 collective-permute-done.1
  503.5 8.0 collective-permute-done.1
  518.5 9.2 %collective-permute-done.1 = bf16[32,4096]{1,0:T(8,128)(2,1)S(1)} collective-permute-done((bf16[32,4096]{1,0:T(8,128)(2,1)S(1)}, bf16[32,4096]{1,0:T(8,128)(2,1)S(1)}, u32[]{:S(2)}, u32[]{:S(2)}) %collective-permute-start.1) | collective-permute-done | bytes 262176 | tf_op jit(solution)/shard_map/while/body/eval_jaxpr/ppermute | solution.py:28
  534.5 6.8 collective-permute-done.1
  548.2 57.5 %collective-permute-done.1 = bf16[32,4096]{1,0:T(8,128)(2,1)S(1)} collective-permute-done((bf16[32,4096]{1,0:T(8,128)(2,1)S(1)}, bf16[32,4096]{1,0:T(8,128)(2,1)S(1)}, u32[]{:S(2)}, u32[]{:S(2)}) %collective-permute-start.1) | collective-permute-done | bytes 262176 | tf_op jit(solution)/shard_map/while/body/eval_jaxpr/ppermute | solution.py:28
  606.9 10.9 %conditional.5 = (bf16[32,4096]{1,0:T(8,128)(2,1)S(1)}, bf16[32,512]{1,0:T(8,128)(2,1)S(1)}, bf16[32,128]{1,0:T(8,128)(2,1)}) conditional(s32[]{:T(128)} %convert_element_type.80, () %tuple.85, (pred[]{:T(512)}, s32[6]{0:T(128)S(1)}, s32[]{:T(128)}, bf16[6,32,4096]{2,1,0:T(8,128)(2,1)}, bf16[32,4096]{1,0:T(8,128)(2,1)S(1)}, ...), branch_computations={%region_6.6_spmd, %region_7.8_spmd} | conditional | flops 308170752 | bytes 30656048 | solution.py:154
  628.6 10.9 %conditional.5 = (bf16[32,4096]{1,0:T(8,128)(2,1)S(1)}, bf16[32,512]{1,0:T(8,128)(2,1)S(1)}, bf16[32,128]{1,0:T(8,128)(2,1)}) conditional(s32[]{:T(128)} %convert_element_type.80, () %tuple.85, (pred[]{:T(512)}, s32[6]{0:T(128)S(1)}, s32[]{:T(128)}, bf16[6,32,4096]{2,1,0:T(8,128)(2,1)}, bf16[32,4096]{1,0:T(8,128)(2,1)S(1)}, ...), branch_computations={%region_6.6_spmd, %region_7.8_spmd} | conditional | flops 308170752 | bytes 30656048 | solution.py:154
  650.3 10.9 %conditional.5 = (bf16[32,4096]{1,0:T(8,128)(2,1)S(1)}, bf16[32,512]{1,0:T(8,128)(2,1)S(1)}, bf16[32,128]{1,0:T(8,128)(2,1)}) conditional(s32[]{:T(128)} %convert_element_type.80, () %tuple.85, (pred[]{:T(512)}, s32[6]{0:T(128)S(1)}, s32[]{:T(128)}, bf16[6,32,4096]{2,1,0:T(8,128)(2,1)}, bf16[32,4096]{1,0:T(8,128)(2,1)S(1)}, ...), branch_computations={%region_6.6_spmd, %region_7.8_spmd} | conditional | flops 308170752 | bytes 30656048 | solution.py:154
  672.0 10.9 %conditional.5 = (bf16[32,4096]{1,0:T(8,128)(2,1)S(1)}, bf16[32,512]{1,0:T(8,128)(2,1)S(1)}, bf16[32,128]{1,0:T(8,128)(2,1)}) conditional(s32[]{:T(128)} %convert_element_type.80, () %tuple.85, (pred[]{:T(512)}, s32[6]{0:T(128)S(1)}, s32[]{:T(128)}, bf16[6,32,4096]{2,1,0:T(8,128)(2,1)}, bf16[32,4096]{1,0:T(8,128)(2,1)S(1)}, ...), branch_computations={%region_6.6_spmd, %region_7.8_spmd} | conditional | flops 308170752 | bytes 30656048 | solution.py:154
  688.6 4.7 collective-permute-done.1
  694.6 10.9 %conditional.5 = (bf16[32,4096]{1,0:T(8,128)(2,1)S(1)}, bf16[32,512]{1,0:T(8,128)(2,1)S(1)}, bf16[32,128]{1,0:T(8,128)(2,1)}) conditional(s32[]{:T(128)} %convert_element_type.80, () %tuple.85, (pred[]{:T(512)}, s32[6]{0:T(128)S(1)}, s32[]{:T(128)}, bf16[6,32,4096]{2,1,0:T(8,128)(2,1)}, bf16[32,4096]{1,0:T(8,128)(2,1)S(1)}, ...), branch_computations={%region_6.6_spmd, %region_7.8_spmd} | conditional | flops 308170752 | bytes 30656048 | solution.py:154
  711.2 6.4 collective-permute-done.1
  718.8 10.9 %conditional.5 = (bf16[32,4096]{1,0:T(8,128)(2,1)S(1)}, bf16[32,512]{1,0:T(8,128)(2,1)S(1)}, bf16[32,128]{1,0:T(8,128)(2,1)}) conditional(s32[]{:T(128)} %convert_element_type.80, () %tuple.85, (pred[]{:T(512)}, s32[6]{0:T(128)S(1)}, s32[]{:T(128)}, bf16[6,32,4096]{2,1,0:T(8,128)(2,1)}, bf16[32,4096]{1,0:T(8,128)(2,1)S(1)}, ...), branch_computations={%region_6.6_spmd, %region_7.8_spmd} | conditional | flops 308170752 | bytes 30656048 | solution.py:154
  735.5 6.0 collective-permute-done.1
  743.3 12.2 %collective-permute-start.1 = (bf16[32,4096]{1,0:T(8,128)(2,1)S(1)}, bf16[32,4096]{1,0:T(8,128)(2,1)S(1)}, u32[]{:S(2)}, u32[]{:S(2)}) collective-permute-start(bf16[32,4096]{1,0:T(8,128)(2,1)S(1)} %get-tuple-element.797), channel_id=1, source_target_pairs={{64,0},{128,64},{192,128},{256,192},{320,256},{384,320},{448,384},... | collective-permute-start | bytes 786440 | tf_op jit(solution)/shard_map/while/body/eval_jaxpr/ppermute | solution.py:28
  764.5 92.7 %all_to_all.5 = bf16[64,72,128]{2,1,0:T(8,128)(2,1)S(1)} all-to-all(bf16[64,72,128]{2,1,0:T(8,128)(2,1)S(1)} %pad_maximum_fusion), channel_id=1, replica_groups=mesh['section'=8,'fsdp'=64] {'fsdp'}, dimensions={0} | all-to-all | bytes 2359296 | tf_op jit(solution)/shard_map/all_to_all | solution.py:39
  (495 shorter events, 307.3 us)
Async XLA Ops:
  7.2 138.4 %all-gather.3.cloned.1.call-start = ((), (), s32[]{:S(2)}) async-start(), calls=%async_computation.1 | async-start | bytes 9717760 | tf_op jit(solution)/shard_map/all_gather | solution.py:17
  156.9 5.8 slice-start
  206.6 15.5 %collective-permute-start = (bf16[32,4096]{1,0:T(8,128)(2,1)}, bf16[32,4096]{1,0:T(8,128)(2,1)S(1)}, u32[]{:S(2)}, u32[]{:S(2)}) collective-permute-start(bf16[32,4096]{1,0:T(8,128)(2,1)} %get-tuple-element.776), channel_id=1, source_target_pairs={{0,64},{64,128},{128,192},{192,256},{256,320},{320,384},{384,448},... | collective-permute-start | bytes 786440 | tf_op jit(solution)/shard_map/while/body/eval_jaxpr/ppermute | solution.py:28
  227.3 3.1 copy-start.1
  231.3 3.9 copy-start.2
  235.2 10.6 %collective-permute-start = (bf16[32,4096]{1,0:T(8,128)(2,1)}, bf16[32,4096]{1,0:T(8,128)(2,1)S(1)}, u32[]{:S(2)}, u32[]{:S(2)}) collective-permute-start(bf16[32,4096]{1,0:T(8,128)(2,1)} %get-tuple-element.776), channel_id=1, source_target_pairs={{0,64},{64,128},{128,192},{192,256},{256,320},{320,384},{384,448},... | collective-permute-start | bytes 786440 | tf_op jit(solution)/shard_map/while/body/eval_jaxpr/ppermute | solution.py:28
  251.0 3.1 copy-start.1
  255.0 3.9 copy-start.2
  258.9 9.7 %collective-permute-start = (bf16[32,4096]{1,0:T(8,128)(2,1)}, bf16[32,4096]{1,0:T(8,128)(2,1)S(1)}, u32[]{:S(2)}, u32[]{:S(2)}) collective-permute-start(bf16[32,4096]{1,0:T(8,128)(2,1)} %get-tuple-element.776), channel_id=1, source_target_pairs={{0,64},{64,128},{128,192},{192,256},{256,320},{320,384},{384,448},... | collective-permute-start | bytes 786440 | tf_op jit(solution)/shard_map/while/body/eval_jaxpr/ppermute | solution.py:28
  273.9 3.1 copy-start.1
  277.9 3.9 copy-start.2
  281.8 8.8 %collective-permute-start = (bf16[32,4096]{1,0:T(8,128)(2,1)}, bf16[32,4096]{1,0:T(8,128)(2,1)S(1)}, u32[]{:S(2)}, u32[]{:S(2)}) collective-permute-start(bf16[32,4096]{1,0:T(8,128)(2,1)} %get-tuple-element.776), channel_id=1, source_target_pairs={{0,64},{64,128},{128,192},{192,256},{256,320},{320,384},{384,448},... | collective-permute-start | bytes 786440 | tf_op jit(solution)/shard_map/while/body/eval_jaxpr/ppermute | solution.py:28
  295.8 3.1 copy-start.1
  299.8 3.9 copy-start.2
  303.7 9.3 %collective-permute-start = (bf16[32,4096]{1,0:T(8,128)(2,1)}, bf16[32,4096]{1,0:T(8,128)(2,1)S(1)}, u32[]{:S(2)}, u32[]{:S(2)}) collective-permute-start(bf16[32,4096]{1,0:T(8,128)(2,1)} %get-tuple-element.776), channel_id=1, source_target_pairs={{0,64},{64,128},{128,192},{192,256},{256,320},{320,384},{384,448},... | collective-permute-start | bytes 786440 | tf_op jit(solution)/shard_map/while/body/eval_jaxpr/ppermute | solution.py:28
  318.2 3.1 copy-start.1
  322.2 3.9 copy-start.2
  326.1 9.8 %collective-permute-start = (bf16[32,4096]{1,0:T(8,128)(2,1)}, bf16[32,4096]{1,0:T(8,128)(2,1)S(1)}, u32[]{:S(2)}, u32[]{:S(2)}) collective-permute-start(bf16[32,4096]{1,0:T(8,128)(2,1)} %get-tuple-element.776), channel_id=1, source_target_pairs={{0,64},{64,128},{128,192},{192,256},{256,320},{320,384},{384,448},... | collective-permute-start | bytes 786440 | tf_op jit(solution)/shard_map/while/body/eval_jaxpr/ppermute | solution.py:28
  341.1 3.1 copy-start.1
  345.1 3.9 copy-start.2
  349.0 9.7 %collective-permute-start = (bf16[32,4096]{1,0:T(8,128)(2,1)}, bf16[32,4096]{1,0:T(8,128)(2,1)S(1)}, u32[]{:S(2)}, u32[]{:S(2)}) collective-permute-start(bf16[32,4096]{1,0:T(8,128)(2,1)} %get-tuple-element.776), channel_id=1, source_target_pairs={{0,64},{64,128},{128,192},{192,256},{256,320},{320,384},{384,448},... | collective-permute-start | bytes 786440 | tf_op jit(solution)/shard_map/while/body/eval_jaxpr/ppermute | solution.py:28
  364.9 16.4 %collective-permute-start = (bf16[32,4096]{1,0:T(8,128)(2,1)}, bf16[32,4096]{1,0:T(8,128)(2,1)S(1)}, u32[]{:S(2)}, u32[]{:S(2)}) collective-permute-start(bf16[32,4096]{1,0:T(8,128)(2,1)} %get-tuple-element.776), channel_id=1, source_target_pairs={{0,64},{64,128},{128,192},{192,256},{256,320},{320,384},{384,448},... | collective-permute-start | bytes 786440 | tf_op jit(solution)/shard_map/while/body/eval_jaxpr/ppermute | solution.py:28
  387.6 9.7 %collective-permute-start = (bf16[32,4096]{1,0:T(8,128)(2,1)}, bf16[32,4096]{1,0:T(8,128)(2,1)S(1)}, u32[]{:S(2)}, u32[]{:S(2)}) collective-permute-start(bf16[32,4096]{1,0:T(8,128)(2,1)} %get-tuple-element.776), channel_id=1, source_target_pairs={{0,64},{64,128},{128,192},{192,256},{256,320},{320,384},{384,448},... | collective-permute-start | bytes 786440 | tf_op jit(solution)/shard_map/while/body/eval_jaxpr/ppermute | solution.py:28
  403.6 11.5 %collective-permute-start = (bf16[32,4096]{1,0:T(8,128)(2,1)}, bf16[32,4096]{1,0:T(8,128)(2,1)S(1)}, u32[]{:S(2)}, u32[]{:S(2)}) collective-permute-start(bf16[32,4096]{1,0:T(8,128)(2,1)} %get-tuple-element.776), channel_id=1, source_target_pairs={{0,64},{64,128},{128,192},{192,256},{256,320},{320,384},{384,448},... | collective-permute-start | bytes 786440 | tf_op jit(solution)/shard_map/while/body/eval_jaxpr/ppermute | solution.py:28
  421.3 9.7 %collective-permute-start = (bf16[32,4096]{1,0:T(8,128)(2,1)}, bf16[32,4096]{1,0:T(8,128)(2,1)S(1)}, u32[]{:S(2)}, u32[]{:S(2)}) collective-permute-start(bf16[32,4096]{1,0:T(8,128)(2,1)} %get-tuple-element.776), channel_id=1, source_target_pairs={{0,64},{64,128},{128,192},{192,256},{256,320},{320,384},{384,448},... | collective-permute-start | bytes 786440 | tf_op jit(solution)/shard_map/while/body/eval_jaxpr/ppermute | solution.py:28
  437.3 13.2 %collective-permute-start = (bf16[32,4096]{1,0:T(8,128)(2,1)}, bf16[32,4096]{1,0:T(8,128)(2,1)S(1)}, u32[]{:S(2)}, u32[]{:S(2)}) collective-permute-start(bf16[32,4096]{1,0:T(8,128)(2,1)} %get-tuple-element.776), channel_id=1, source_target_pairs={{0,64},{64,128},{128,192},{192,256},{256,320},{320,384},{384,448},... | collective-permute-start | bytes 786440 | tf_op jit(solution)/shard_map/while/body/eval_jaxpr/ppermute | solution.py:28
  456.8 9.7 %collective-permute-start = (bf16[32,4096]{1,0:T(8,128)(2,1)}, bf16[32,4096]{1,0:T(8,128)(2,1)S(1)}, u32[]{:S(2)}, u32[]{:S(2)}) collective-permute-start(bf16[32,4096]{1,0:T(8,128)(2,1)} %get-tuple-element.776), channel_id=1, source_target_pairs={{0,64},{64,128},{128,192},{192,256},{256,320},{320,384},{384,448},... | collective-permute-start | bytes 786440 | tf_op jit(solution)/shard_map/while/body/eval_jaxpr/ppermute | solution.py:28
  470.4 11.6 %collective-permute-start.1 = (bf16[32,4096]{1,0:T(8,128)(2,1)S(1)}, bf16[32,4096]{1,0:T(8,128)(2,1)S(1)}, u32[]{:S(2)}, u32[]{:S(2)}) collective-permute-start(bf16[32,4096]{1,0:T(8,128)(2,1)S(1)} %get-tuple-element.797), channel_id=1, source_target_pairs={{64,0},{128,64},{192,128},{256,192},{320,256},{384,320},{448,384},... | collective-permute-start | bytes 786440 | tf_op jit(solution)/shard_map/while/body/eval_jaxpr/ppermute | solution.py:28
  483.9 12.8 %collective-permute-start.1 = (bf16[32,4096]{1,0:T(8,128)(2,1)S(1)}, bf16[32,4096]{1,0:T(8,128)(2,1)S(1)}, u32[]{:S(2)}, u32[]{:S(2)}) collective-permute-start(bf16[32,4096]{1,0:T(8,128)(2,1)S(1)} %get-tuple-element.797), channel_id=1, source_target_pairs={{64,0},{128,64},{192,128},{256,192},{320,256},{384,320},{448,384},... | collective-permute-start | bytes 786440 | tf_op jit(solution)/shard_map/while/body/eval_jaxpr/ppermute | solution.py:28
  498.5 13.0 %collective-permute-start.1 = (bf16[32,4096]{1,0:T(8,128)(2,1)S(1)}, bf16[32,4096]{1,0:T(8,128)(2,1)S(1)}, u32[]{:S(2)}, u32[]{:S(2)}) collective-permute-start(bf16[32,4096]{1,0:T(8,128)(2,1)S(1)} %get-tuple-element.797), channel_id=1, source_target_pairs={{64,0},{128,64},{192,128},{256,192},{320,256},{384,320},{448,384},... | collective-permute-start | bytes 786440 | tf_op jit(solution)/shard_map/while/body/eval_jaxpr/ppermute | solution.py:28
  513.5 14.2 %collective-permute-start.1 = (bf16[32,4096]{1,0:T(8,128)(2,1)S(1)}, bf16[32,4096]{1,0:T(8,128)(2,1)S(1)}, u32[]{:S(2)}, u32[]{:S(2)}) collective-permute-start(bf16[32,4096]{1,0:T(8,128)(2,1)S(1)} %get-tuple-element.797), channel_id=1, source_target_pairs={{64,0},{128,64},{192,128},{256,192},{320,256},{384,320},{448,384},... | collective-permute-start | bytes 786440 | tf_op jit(solution)/shard_map/while/body/eval_jaxpr/ppermute | solution.py:28
  529.5 11.8 %collective-permute-start.1 = (bf16[32,4096]{1,0:T(8,128)(2,1)S(1)}, bf16[32,4096]{1,0:T(8,128)(2,1)S(1)}, u32[]{:S(2)}, u32[]{:S(2)}) collective-permute-start(bf16[32,4096]{1,0:T(8,128)(2,1)S(1)} %get-tuple-element.797), channel_id=1, source_target_pairs={{64,0},{128,64},{192,128},{256,192},{320,256},{384,320},{448,384},... | collective-permute-start | bytes 786440 | tf_op jit(solution)/shard_map/while/body/eval_jaxpr/ppermute | solution.py:28
  543.2 62.4 %collective-permute-start.1 = (bf16[32,4096]{1,0:T(8,128)(2,1)S(1)}, bf16[32,4096]{1,0:T(8,128)(2,1)S(1)}, u32[]{:S(2)}, u32[]{:S(2)}) collective-permute-start(bf16[32,4096]{1,0:T(8,128)(2,1)S(1)} %get-tuple-element.797), channel_id=1, source_target_pairs={{64,0},{128,64},{192,128},{256,192},{320,256},{384,320},{448,384},... | collective-permute-start | bytes 786440 | tf_op jit(solution)/shard_map/while/body/eval_jaxpr/ppermute | solution.py:28
  609.5 3.8 copy-start
  617.8 9.5 %collective-permute-start.1 = (bf16[32,4096]{1,0:T(8,128)(2,1)S(1)}, bf16[32,4096]{1,0:T(8,128)(2,1)S(1)}, u32[]{:S(2)}, u32[]{:S(2)}) collective-permute-start(bf16[32,4096]{1,0:T(8,128)(2,1)S(1)} %get-tuple-element.797), channel_id=1, source_target_pairs={{64,0},{128,64},{192,128},{256,192},{320,256},{384,320},{448,384},... | collective-permute-start | bytes 786440 | tf_op jit(solution)/shard_map/while/body/eval_jaxpr/ppermute | solution.py:28
  631.2 3.8 copy-start
  639.5 9.5 %collective-permute-start.1 = (bf16[32,4096]{1,0:T(8,128)(2,1)S(1)}, bf16[32,4096]{1,0:T(8,128)(2,1)S(1)}, u32[]{:S(2)}, u32[]{:S(2)}) collective-permute-start(bf16[32,4096]{1,0:T(8,128)(2,1)S(1)} %get-tuple-element.797), channel_id=1, source_target_pairs={{64,0},{128,64},{192,128},{256,192},{320,256},{384,320},{448,384},... | collective-permute-start | bytes 786440 | tf_op jit(solution)/shard_map/while/body/eval_jaxpr/ppermute | solution.py:28
  652.9 3.8 copy-start
  661.2 9.5 %collective-permute-start.1 = (bf16[32,4096]{1,0:T(8,128)(2,1)S(1)}, bf16[32,4096]{1,0:T(8,128)(2,1)S(1)}, u32[]{:S(2)}, u32[]{:S(2)}) collective-permute-start(bf16[32,4096]{1,0:T(8,128)(2,1)S(1)} %get-tuple-element.797), channel_id=1, source_target_pairs={{64,0},{128,64},{192,128},{256,192},{320,256},{384,320},{448,384},... | collective-permute-start | bytes 786440 | tf_op jit(solution)/shard_map/while/body/eval_jaxpr/ppermute | solution.py:28
  674.6 3.8 copy-start
  682.9 10.4 %collective-permute-start.1 = (bf16[32,4096]{1,0:T(8,128)(2,1)S(1)}, bf16[32,4096]{1,0:T(8,128)(2,1)S(1)}, u32[]{:S(2)}, u32[]{:S(2)}) collective-permute-start(bf16[32,4096]{1,0:T(8,128)(2,1)S(1)} %get-tuple-element.797), channel_id=1, source_target_pairs={{64,0},{128,64},{192,128},{256,192},{320,256},{384,320},{448,384},... | collective-permute-start | bytes 786440 | tf_op jit(solution)/shard_map/while/body/eval_jaxpr/ppermute | solution.py:28
  697.1 3.8 copy-start
  705.5 12.1 %collective-permute-start.1 = (bf16[32,4096]{1,0:T(8,128)(2,1)S(1)}, bf16[32,4096]{1,0:T(8,128)(2,1)S(1)}, u32[]{:S(2)}, u32[]{:S(2)}) collective-permute-start(bf16[32,4096]{1,0:T(8,128)(2,1)S(1)} %get-tuple-element.797), channel_id=1, source_target_pairs={{64,0},{128,64},{192,128},{256,192},{320,256},{384,320},{448,384},... | collective-permute-start | bytes 786440 | tf_op jit(solution)/shard_map/while/body/eval_jaxpr/ppermute | solution.py:28
  721.4 3.8 copy-start
  729.8 11.7 %collective-permute-start.1 = (bf16[32,4096]{1,0:T(8,128)(2,1)S(1)}, bf16[32,4096]{1,0:T(8,128)(2,1)S(1)}, u32[]{:S(2)}, u32[]{:S(2)}) collective-permute-start(bf16[32,4096]{1,0:T(8,128)(2,1)S(1)} %get-tuple-element.797), channel_id=1, source_target_pairs={{64,0},{128,64},{192,128},{256,192},{320,256},{384,320},{448,384},... | collective-permute-start | bytes 786440 | tf_op jit(solution)/shard_map/while/body/eval_jaxpr/ppermute | solution.py:28
  743.3 16.7 %collective-permute-start.1 = (bf16[32,4096]{1,0:T(8,128)(2,1)S(1)}, bf16[32,4096]{1,0:T(8,128)(2,1)S(1)}, u32[]{:S(2)}, u32[]{:S(2)}) collective-permute-start(bf16[32,4096]{1,0:T(8,128)(2,1)S(1)} %get-tuple-element.797), channel_id=1, source_target_pairs={{64,0},{128,64},{192,128},{256,192},{320,256},{384,320},{448,384},... | collective-permute-start | bytes 786440 | tf_op jit(solution)/shard_map/while/body/eval_jaxpr/ppermute | solution.py:28
  760.2 3.2 copy-start.5
  760.2 3.4 copy-start.6
  (14 other events, 25.6 us)
Sparse Core Ops, SparseCore 0:
  11.6 133.9 all-gather.2
where the time goes:
time: 875 us; the launch traced here: 865 us
  waiting for transfers between devices  280 us (32%)
  local copies, waits for them, and re-layouts  148 us (17%)
  starting transfers between devices  114 us (13%)
  blocking collectives  92.7 us (11%)
  matrix products  90.8 us (10%)
  other arithmetic  68.9 us (8%)
  loops' own time  56 us (6%)
  between operations  14.2 us (2%)
    ppermute x26, waiting for transfers between devices, from_behind(): return lax.ppermute(block, axis, route)  146 us
    all_gather x1, waiting for transfers between devices, gather_packed(): lines, at, gathered = (lax.all_gather(ravelled, axis), 0, [])  134 us
    ppermute x26, starting transfers between devices, from_behind(): return lax.ppermute(block, axis, route)  114 us
    all_to_all x1, blocking collectives, sum_at_owner(): lax.all_to_all(split_up(value, dim, devices), axis, 0, 0, tiled=True)  92.7 us
    dynamic_update_slice x91, other arithmetic, store(): lax.dynamic_update_index_in_dim(buffer, jnp.where(in_range, item, previou...  58.3 us
    dynamic_slice x78, local copies, waits for them, and re-layouts, store(): previous = lax.dynamic_index_in_dim(buffer, clipped, 0, keepdims=False)  43.8 us
    another operation x1, loops' own time, body(): carried, unused = lax.scan(forward_step, start_fwd, moments)  34.5 us
    dot_general x6, matrix products, layer_forward(): jnp.dot(values, w_proj, preferred_element_type=jnp.float32)  23.3 us
  transfers between devices with their start and end apart: 27, of which 24 were waited for; matrix products, arithmetic and copies ran while one was open for 10% of the time, Pallas kernels for 0%

commit v1 on v0

v1 whole, which is shorter than its diff:
```python
import functools

import jax
import jax.numpy as jnp
from jax import lax
from jax.experimental import pallas as pl
from jax.experimental.pallas import tpu as pltpu
from jax.sharding import PartitionSpec as P

EPS = 1e-05
MESH = pl.DeviceIdType.MESH
F32 = jnp.float32
BF16 = jnp.bfloat16
NT = (((1,), (1,)), ((), ()))
TN = (((0,), (0,)), ((), ()))
NY = 4
PIECES = 4


def dot(a, b):
    return jnp.dot(a, b, preferred_element_type=F32)


def dot_nt(a, b):
    return lax.dot_general(a, b, NT, preferred_element_type=F32)


class Dims:
    def __init__(self, mesh, rows, width, hv):
        self.nx = mesh.shape["section"] // 2
        self.nz = mesh.shape["fsdp"] // 4
        self.nh = self.nz // 2
        self.rows = rows
        self.d = width
        self.hv = hv
        self.hb = hv // 128
        self.off_out = 64 * self.hb
        self.off_down = 128 * self.hb
        self.off_up = self.off_down + 64
        self.shard = self.off_up + 16
        tiles = self.shard // 16
        self.rp = (tiles * 351 // 1000 + 1) * 16 if tiles < 37 else 208
        self.half = max((tiles + 1) // 2 * 16, self.rp)
        self.qa = self.rp + (tiles - self.rp // 16) // 2 * 16


def kernel(dm, shard, tok, cot, out, gout, buf, xs, ns, iv, lo, gs, dv, dl, up, dn, rr, rc, s1, t1, t2, v1, v2, s2,
           zb, zr, yr, ss, cs, fr, fs, br, bs, os, gsm, zrr):
    nx, nz, nh, d_all, hv, hb = dm.nx, dm.nz, dm.nh, dm.d, dm.hv, dm.hb
    sec = lax.axis_index("section")
    fid = lax.axis_index("fsdp")
    x = sec // 2
    yh = sec % 2
    z = fid // 4
    y = yh * 2 + (fid // 2) % 2
    c = fid % 2
    yp, ym, yo = (y + 1) % NY, (y + NY - 1) % NY, (y + 2) % NY
    zp, zm = (z + 1) % nz, (z + nz - 1) % nz

    def dev(x_, y_, z_, c_):
        return (x_ * 2 + y_ // 2, z_ * 4 + (y_ % 2) * 2 + c_)

    def slot(y_, z_, c_):
        return (y_ // 2) * (4 * nz) + z_ * 4 + (y_ % 2) * 2 + c_

    d_zp, d_zm = dev(x, y, zp, c), dev(x, y, zm, c)
    d_yp, d_ym, d_yo = dev(x, yp, z, c), dev(x, ym, z, c), dev(x, yo, z, c)
    d_sib = dev(x, y, z, 1 - c)
    d_xp, d_xm = dev(x + 1, y, z, c), dev(x - 1, y, z, c)

    def send(src, dst, ssem, rsem, to):
        pltpu.make_async_remote_copy(
            src_ref=src, dst_ref=dst, send_sem=ssem, recv_sem=rsem, device_id=to, device_id_type=MESH
        ).start()

    def got(ref, rsem):
        pltpu.make_async_remote_copy(
            src_ref=ref, dst_ref=ref, send_sem=rsem, recv_sem=rsem, device_id=d_sib, device_id_type=MESH
        ).wait_recv()

    def left(ref, ssem):
        pltpu.make_async_remote_copy(
            src_ref=ref, dst_ref=ref, send_sem=ssem, recv_sem=ssem, device_id=d_sib, device_id_type=MESH
        ).wait_send()

    barrier = pltpu.get_barrier_semaphore()

    def greet(to):
        pl.semaphore_signal(barrier, inc=1, device_id=to, device_id_type=MESH)

    for to in (d_sib, d_yp, d_ym, d_yo):
        greet(to)

    def greet_z(i, _):
        greet(dev(x, y, (z + i) % nz, c))
        return _

    lax.fori_loop(1, nz, greet_z, 0)

    greet(dev((x + nx - 1) % nx, y, z, c))
    greet(dev((x + 1) % nx, y, z, c))
    pl.semaphore_wait(barrier, 4 + nz - 1 + 2)

    rows, rp, half, qa = dm.shard, dm.rp, dm.half, dm.qa

    def part(s, r0, r1):
        return buf.at[s, pl.ds(r0, r1 - r0), :]

    def to_sib(s, r0, r1):
        send(part(s, r0, r1), part(s, r0, r1), cs.at[0], cs.at[1], d_sib)

    def move(s, r0, r1, ssem, rsem, to):
        send(part(s, r0, r1), part(s, r0, r1), ssem, rsem, to)

    me = slot(y, z, c)
    own = buf.at[me]
    send(shard, own, ss.at[0], zr.at[0, 1, 0], d_zp)
    if nh > 1:
        send(shard, own, ss.at[1], zr.at[1, 1, 0], d_zm)
    send(shard, own, ss.at[4], yr.at[0, 0], d_yp)
    send(shard, own, ss.at[11], yr.at[0, 1], d_ym)
    send(shard, own, cs.at[0], cs.at[1], d_sib)
    local = pltpu.make_async_copy(shard, own, cs.at[2])
    local.start()

    def send_p(s, kind, dist_of):
        for way, (ps, to) in enumerate(((2, d_zp), (3, d_zm))):
            if way == 0 or nh > 1:
                move(s, 0, rp, ss.at[ps], zr.at[way, dist_of, kind], to)

    s_m, s_p, s_o = slot(ym, z, c), slot(yp, z, c), slot(yo, z, c)
    got(part(s_m, 0, rows), yr.at[0, 0])
    move(s_m, 0, half, ss.at[5], yr.at[0, 2], d_yp)
    send_p(s_m, 2, 1)
    to_sib(s_m, 0, rows)
    got(part(s_p, 0, rows), yr.at[0, 1])
    move(s_p, half, rows, ss.at[6], yr.at[0, 3], d_ym)
    send_p(s_p, 1, 1)
    to_sib(s_p, 0, rows)

    def z_from(way, d):
        return (z + nz - d) % nz if way == 0 else (z + d) % nz

    def e_of(way, d):
        return d if way == 0 else nh + d

    def limit(way):
        return nh if way == 0 else nh - 1

    def z_shard(way, d):
        s = slot(y, z_from(way, d), c)
        e = e_of(way, d)
        got(part(s, 0, rows), zr.at[way, d, 0])

        @pl.when(d < limit(way))
        def _():
            move(s, 0, rows, ss.at[way], zr.at[way, d + 1, 0], (d_zp, d_zm)[way])

        move(s, rp, rows, ss.at[7], yr.at[e, 0], d_yp)
        move(s, rp, rows, ss.at[8], yr.at[e, 1], d_ym)
        to_sib(s, 0, rows)

    def z_parts(way, d):
        for kind, col in ((2, ym), (1, yp), (3, yo)):
            s = slot(col, z_from(way, d), c)
            got(part(s, 0, rp), zr.at[way, d, kind])

            @pl.when(d < limit(way))
            def _(s=s, kind=kind):
                move(s, 0, rp, ss.at[2 + way], zr.at[way, d + 1, kind], (d_zp, d_zm)[way])

            to_sib(s, 0, rp)

    def y_near(way, d):
        e, zz = e_of(way, d), z_from(way, d)
        a, b = slot(ym, zz, c), slot(yp, zz, c)
        got(part(a, rp, rows), yr.at[e, 0])
        move(a, rp, qa, ss.at[9], yr.at[e, 2], d_yp)
        to_sib(a, rp, rows)
        got(part(b, rp, rows), yr.at[e, 1])
        move(b, qa, rows, ss.at[10], yr.at[e, 3], d_ym)
        to_sib(b, rp, rows)

    def y_far(way, d):
        e, zz = e_of(way, d), z_from(way, d)
        s = slot(yo, zz, c)
        got(part(s, rp, qa), yr.at[e, 2])
        to_sib(s, rp, qa)
        got(part(s, qa, rows), yr.at[e, 3])
        to_sib(s, qa, rows)

    def gather_step(d, carry):
        for way in (0, 1):
            pl.when(d <= limit(way))(functools.partial(z_shard, way, d))

        @pl.when(d == 1)
        def _():
            got(part(s_o, 0, half), yr.at[0, 2])
            send_p(s_o, 3, 1)
            to_sib(s_o, 0, half)
            got(part(s_o, half, rows), yr.at[0, 3])
            to_sib(s_o, half, rows)

        for way in (0, 1):
            pl.when(d <= limit(way))(functools.partial(z_parts, way, d))
        for way in (0, 1):
            pl.when((d > 1) & (d <= limit(way) + 1))(functools.partial(y_near, way, d - 1))
        for way in (0, 1):
            pl.when((d > 2) & (d <= limit(way) + 2))(functools.partial(y_far, way, d - 2))
        return carry

    lax.fori_loop(1, nh + 3, gather_step, 0)

    local.wait()
    half_all = buf.at[pl.ds(0, 4 * nz)]
    got(half_all, cs.at[1])
    left(half_all, cs.at[0])

    def span(n, r):
        return buf.at[pl.ds(0, n), pl.ds(0, r), :]

    left(span(nh, rows), ss.at[0])
    left(span(3 * nh, rp), ss.at[2])
    if nh > 1:
        left(span(nh - 1, rows), ss.at[1])
        left(span(3 * (nh - 1), rp), ss.at[3])
    left(span(1, rows), ss.at[4])
    left(span(1, rows), ss.at[11])
    left(span(1, half), ss.at[5])
    left(span(1, rows - half), ss.at[6])
    left(span(nz - 1, rows - rp), ss.at[7])
    left(span(nz - 1, rows - rp), ss.at[8])
    left(span(nz - 1, qa - rp), ss.at[9])
    left(span(nz - 1, rows - qa), ss.at[10])

    for l in range(2):
        raw = buf[pl.ds(l * 4 * nz, 4 * nz), pl.ds(dm.off_up, 16), :].astype(F32)
        up[l] = raw[:, :8, :].reshape(hv, 128).astype(BF16)

    @pl.when(x == 0)
    def _():
        for u in range(3):
            xs[0, u] = tok[u]

    @pl.when(x == nx - 1)
    def _():
        for u in range(3):
            gs[2, u] = cot[u]

    tokens = dm.rows

    def block(l, k, off):
        return buf[pl.ds(l * 4 * nz + 4 * k, 4), pl.ds(off, 64), :].reshape(256, 128)

    def w_in(l, k):
        return jnp.concatenate([block(l, k, 64 * b) for b in range(hb)] + [block(l, k, dm.off_down)], axis=1)

    def w_back(l, k):
        return jnp.concatenate([block(l, k, dm.off_out + 64 * b) for b in range(hb)], axis=1)

    def cols(k):
        return pl.ds(256 * k, 256)

    width = d_all // PIECES
    per_piece = nz // PIECES

    def piece(ref, i, u, p):
        return ref.at[i, u, :, pl.ds(width * p, width)]

    def lanes(v):
        return v[:, :128] + v[:, 128:]

    def run_forward(u):
        @pl.when(x > 0)
        def _():
            for p in range(PIECES):
                got(piece(xs, 0, u, p), fr.at[u, p])

        def layer(l, carry):
            total = jnp.zeros((tokens, 128), F32)
            for k in range(nz):
                v = xs[l, u, :, cols(k)].astype(F32)
                total = total + lanes(v * v)
            inv = lax.rsqrt(jnp.sum(total, axis=-1, keepdims=True) * (1.0 / d_all) + EPS)
            iv[l, u] = jnp.broadcast_to(inv, (tokens, 128))
            for k in range(nz):
                ns[l, u, :, cols(k)] = (xs[l, u, :, cols(k)].astype(F32) * inv).astype(BF16)
            acc = jnp.zeros((tokens, hv + 128), F32)
            for k in range(nz):
                acc = acc + dot(ns[l, u, :, cols(k)], w_in(l, k))
            low = acc[:, hv:].astype(BF16)
            lo[l, u] = low
            val = (acc[:, :hv] + dot_nt(low, up[l])).astype(BF16)

            @pl.when(l + x < nx)
            def _():
                for p in range(PIECES):
                    for k in range(p * per_piece, (p + 1) * per_piece):
                        o = xs[l, u, :, cols(k)].astype(F32) + dot_nt(val, w_back(l, k))
                        xs[l + 1, u, :, cols(k)] = o.astype(BF16)
                    for q in ((p - 1,) if p < PIECES - 1 else (p - 1, p)):
                        if q >= 0:

                            @pl.when(l == 1)
                            def _(q=q):
                                send(piece(xs, 2, u, q), piece(xs, 0, u, q), fs.at[u, q], fr.at[u, q], d_xp)

            return carry

        lax.fori_loop(0, 2, layer, 0)

    def run_backward(u):
        @pl.when(x < nx - 1)
        def _():
            for p in range(PIECES):
                got(piece(gs, 2, u, p), br.at[u, p])

        def layer(i, carry):
            l = 1 - i
            acc = jnp.zeros((tokens, hv), F32)
            for k in range(nz):
                acc = acc + dot(gs[l + 1, u, :, cols(k)], w_back(l, k))
            dvb = acc.astype(BF16)
            dv[l, u] = dvb
            dlb = dot(dvb, up[l]).astype(BF16)
            dl[l, u] = dlb
            both = jnp.concatenate([dvb, dlb], axis=1)
            m = jnp.zeros((tokens, 128), F32)
            for k in range(nz):
                g = dot_nt(both, w_in(l, k))
                dn[:, cols(k)] = g
                m = m + lanes(g * xs[l, u, :, cols(k)].astype(F32))
            mean = jnp.sum(m, axis=-1, keepdims=True) * (1.0 / d_all)
            inv = iv[l, u][:, :1]
            scale = inv * inv * mean
            for p in range(PIECES):
                for k in range(p * per_piece, (p + 1) * per_piece):
                    g = dn[:, cols(k)] - xs[l, u, :, cols(k)].astype(F32) * scale
                    gs[l, u, :, cols(k)] = (gs[l + 1, u, :, cols(k)].astype(F32) + inv * g).astype(BF16)
            for p in range(PIECES):

                @pl.when((l == 0) & (x > 0))
                def _(p=p):
                    send(piece(gs, 0, u, p), piece(gs, 2, u, p), bs.at[u, p], br.at[u, p], d_xm)

            @pl.when(l == yh)
            def _():
                pltpu.make_async_copy(gs.at[l, u], out.at[3 * yh + u], os.at[0, u]).start()

            @pl.when(l != yh)
            def _():
                send(gs.at[l, u], out.at[3 * yh + u], os.at[1, u], os.at[2, u], d_yo)

            return carry

        lax.fori_loop(0, 2, layer, 0)

    last = x // (nx - 1)

    def turn(t, carry):
        u = last * (t // 2) + (1 - last) * (t % 3)
        back = last * (t % 2) + (1 - last) * (t // 3)

        @pl.when(back == 0)
        def _():
            run_forward(u)

        @pl.when(back == 1)
        def _():
            run_backward(u)

        return carry

    lax.fori_loop(0, 6, turn, 0)

    def adapter_grads(l, carry):
        dl_all = dl[l].reshape(3 * tokens, 128)
        lo_all = lo[l].reshape(3 * tokens, 128)
        for k in range(nz):
            n_k = ns[l, :, :, cols(k)].reshape(3 * tokens, 256)
            g = lax.dot_general(n_k, dl_all, TN, preferred_element_type=F32).astype(BF16)
            for q in range(4):
                rr[2 * l + q // 2, k, q % 2, pl.ds(0, 64), :] = g[64 * q : 64 * q + 64]
        dv_all = dv[l].reshape(3 * tokens, hv)
        g = lax.dot_general(dv_all, lo_all, TN, preferred_element_type=F32).reshape(nz, 4, 8, 128)
        for q in range(4):
            g_q = g[:, q]
            padded = jnp.concatenate([g_q, jnp.zeros_like(g_q)], axis=1).astype(BF16)
            rr[2 * l + q // 2, :, q % 2, pl.ds(64, 16), :] = padded
        return carry

    lax.fori_loop(0, 2, adapter_grads, 0)

    send(rr.at[:, :, 1 - c], rc, gsm.at[0], gsm.at[1], d_sib)
    got(rc, gsm.at[1])

    def add_core(i, carry):
        a, b = i // nz, i % nz
        s1[a, b] = (rr[a, b, c].astype(F32) + rc[a, b].astype(F32)).astype(BF16)
        return carry

    lax.fori_loop(0, 4 * nz, add_core, 0)
    lo_z, hi_z = pl.ds(0, nh), pl.ds(nh, nh)
    send(s1.at[yo, lo_z], t1, gsm.at[2], gsm.at[3], d_yp)
    send(s1.at[yo, hi_z], t2, gsm.at[4], gsm.at[5], d_ym)
    got(t1, gsm.at[3])

    def add_near(i, carry):
        s1[yp, i] = (s1[yp, i].astype(F32) + t1[i].astype(F32)).astype(BF16)
        return carry

    lax.fori_loop(0, nh, add_near, 0)
    send(s1.at[yp], v1, gsm.at[6], gsm.at[7], d_yp)
    got(t2, gsm.at[5])

    def add_far(i, carry):
        s1[ym, nh + i] = (s1[ym, nh + i].astype(F32) + t2[i].astype(F32)).astype(BF16)
        return carry

    lax.fori_loop(0, nh, add_far, 0)
    send(s1.at[ym], v2, gsm.at[8], gsm.at[9], d_ym)
    got(v1, gsm.at[7])
    got(v2, gsm.at[9])

    def add_y(i, carry):
        s2[i] = (s1[y, i].astype(F32) + v1[i].astype(F32) + v2[i].astype(F32)).astype(BF16)
        return carry

    lax.fori_loop(0, nz, add_y, 0)

    def z_send(i, carry):
        zz = (z + i) % nz
        send(s2.at[zz], zb.at[i], gsm.at[10], zrr.at[i], dev(x, y, zz, c))
        return carry

    lax.fori_loop(1, nz, z_send, 0)

    def z_add(i, acc):
        got(zb.at[i], zrr.at[i])
        return acc + zb[i].astype(F32)

    gout[...] = lax.fori_loop(1, nz, z_add, s2[z].astype(F32))

    left(zb.at[pl.ds(0, nz - 1)], gsm.at[10])
    left(rc, gsm.at[0])
    left(t1, gsm.at[2])
    left(t2, gsm.at[4])
    left(v1, gsm.at[6])
    left(v2, gsm.at[8])
    for u in range(3):
        for p in range(PIECES):

            @pl.when(x < nx - 1)
            def _(u=u, p=p):
                left(piece(xs, 2, u, p), fs.at[u, p])

            @pl.when(x > 0)
            def _(u=u, p=p):
                left(piece(gs, 0, u, p), bs.at[u, p])

        pltpu.make_async_copy(gs.at[0, u], out.at[3 * yh + u], os.at[0, u]).wait()
        left(gs.at[0, u], os.at[1, u])
        got(out.at[3 * (1 - yh) + u], os.at[2, u])


def run_all(dm, shard, tok, cot):
    nz, d, hv, t = dm.nz, dm.d, dm.hv, dm.rows
    vm = pltpu.VMEM
    dma = pltpu.SemaphoreType.DMA
    return pl.pallas_call(
        functools.partial(kernel, dm),
        out_shape=(
            jax.ShapeDtypeStruct((6, t, d), BF16),
            jax.ShapeDtypeStruct((80, 128), F32),
        ),
        in_specs=[pl.BlockSpec(memory_space=vm)] * 3,
        out_specs=(pl.BlockSpec(memory_space=pl.ANY), pl.BlockSpec(memory_space=vm)),
        scratch_shapes=[
            vm((8 * nz, dm.shard, 128), BF16),
            vm((3, 3, t, d), BF16),
            vm((2, 3, t, d), BF16),
            vm((2, 3, t, 128), F32),
            vm((2, 3, t, 128), BF16),
            vm((3, 3, t, d), BF16),
            vm((2, 3, t, hv), BF16),
            vm((2, 3, t, 128), BF16),
            vm((2, hv, 128), BF16),
            vm((t, d), F32),
            vm((4, nz, 2, 80, 128), BF16),
            vm((4, nz, 80, 128), BF16),
            vm((4, nz, 80, 128), BF16),
            vm((dm.nh, 80, 128), BF16),
            vm((dm.nh, 80, 128), BF16),
            vm((nz, 80, 128), BF16),
            vm((nz, 80, 128), BF16),
            vm((nz, 80, 128), BF16),
            vm((nz, 80, 128), BF16),
            dma((2, dm.nh + 2, 4)),
            dma((nz, 4)),
            dma((12,)),
            dma((3,)),
            dma((3, PIECES)),
            dma((3, PIECES)),
            dma((3, PIECES)),
            dma((3, PIECES)),
            dma((3, 3)),
            dma((11,)),
            dma((nz,)),
        ],
        compiler_params=pltpu.CompilerParams(
            collective_id=0, has_side_effects=True, vmem_limit_bytes=60 * 1024 * 1024
        ),
        name="relay",
    )(shard, tok, cot)


def lane_blocks(a):
    return jnp.swapaxes(a.reshape(a.shape[0], -1, 128), 0, 1).reshape(-1, 128)


def solution(mesh):
    def body(tokens, cotangent, order, w_value, w_out, adapter_down, adapter_up):
        dm = Dims(mesh, tokens.shape[1], tokens.shape[2], w_value.shape[2])
        up_t = adapter_up[0].T
        shard = jnp.concatenate(
            [
                lane_blocks(w_value[0]),
                lane_blocks(w_out[0].T),
                adapter_down[0],
                up_t,
                jnp.zeros_like(up_t),
            ],
            axis=0,
        )
        half = lax.axis_index("section") % 2
        mine = lax.dynamic_slice(order, (3 * half,), (3,))
        dx, grads = run_all(dm, shard, tokens[mine], cotangent[mine])
        return (dx[None], grads[:64][None], grads[64:72].T[None])

    return jax.shard_map(
        body,
        mesh=mesh,
        in_specs=(
            P(None, "fsdp", None),
            P(None, "fsdp", None),
            P(),
            P("section", "fsdp", None),
            P("section", None, "fsdp"),
            P("section", "fsdp", None),
            P("section", None, "fsdp"),
        ),
        out_specs=(
            P("section", None, "fsdp", None),
            P("section", "fsdp", None),
            P("section", None, "fsdp"),
        ),
        check_vma=False,
    )
```

time: 875 us -> 231 us (0.26)
  waiting for transfers between devices: 280 us -> 0 us
  Pallas kernels: 0 us -> 217 us
  local copies, waits for them, and re-layouts: 148 us -> 11.6 us
  starting transfers between devices: 114 us -> 0 us
  blocking collectives: 92.7 us -> 0 us
  matrix products: 90.8 us -> 0 us
  other arithmetic: 68.9 us -> 0.89 us
  loops' own time: 56 us -> 0 us
  between operations: 14.2 us -> 0.7 us
    pallas_call x0 -> x1, Pallas kernels: none -> 217 us  [run_all(): pl.pallas_call(functools.partial(kernel, dm), out_shape=(jax.ShapeDtypeSt...]
    ppermute x26 -> x0, waiting for transfers between devices: 146 us -> none  [from_behind(): return lax.ppermute(block, axis, route)]
    all_gather x1 -> x0, waiting for transfers between devices: 134 us -> none  [gather_packed(): lines, at, gathered = (lax.all_gather(ravelled, axis), 0, [])]
    ppermute x26 -> x0, starting transfers between devices: 114 us -> none  [from_behind(): return lax.ppermute(block, axis, route)]
    all_to_all x1 -> x0, blocking collectives: 92.7 us -> none  [sum_at_owner(): lax.all_to_all(split_up(value, dim, devices), axis, 0, 0, tiled=True)]
    dot_general x44 -> x0, matrix products: 90.8 us -> none  [the longest x6 23.3 us: layer_forward(): jnp.dot(values, w_proj, preferred_element_type=jnp.float32)]
    dynamic_slice x123 -> x0, local copies, waits for them, and re-layouts: 70.2 us -> none  [the longest x78 43.8 us: store(): previous = lax.dynamic_index_in_dim(buffer, clipped, 0, keepdims=False)]
    dynamic_update_slice x91 -> x0, other arithmetic: 58.3 us -> none  [store(): lax.dynamic_update_index_in_dim(buffer, jnp.where(in_range, item, previou...]
  transfers between devices with their start and end apart: 27 -> 0, of which waited for: 24 -> 0; matrix products, arithmetic and copies ran while one was open for 10% -> 0% of each run, Pallas kernels for 0% -> 0%
where the time goes in v1:
time: 231 us; the launch traced here: 230 us
  Pallas kernels  217 us (94%)
  local copies, waits for them, and re-layouts  11.6 us (5%)
    pallas_call x1, Pallas kernels, run_all(): pl.pallas_call(functools.partial(kernel, dm), out_shape=(jax.ShapeDtypeSt...  217 us

profile of v1, /device:TPU:25, one launch (start us, length us, event | category | flops | bytes accessed | tf_op | source)
XLA Modules:
  0.0 230.0 jit_solution(6976279960463885627)
XLA Ops:
  0.6 0.0 copy-start
  0.6 0.0 copy-start.1
  0.7 0.9 compare_select_fusion
  1.6 0.9 reshape_squeeze.3
  2.5 0.9 copy_bitcast_fusion
  3.4 0.7 bitcast_dynamic-update-slice_fusion
  4.1 0.7 constant_dynamic-update-slice_fusion.1
  4.8 0.0 copy-done
  4.8 0.0 copy-start.2
  4.8 1.5 gather_fusion.1
  6.3 0.0 copy-done.1
  6.3 1.5 gather_fusion
  7.8 0.0 copy-done.2
  7.8 216.8 %relay.1 = (bf16[6,32,4096]{2,1,0:T(8,128)(2,1)}, f32[80,128]{1,0:T(8,128)}) custom-call(bf16[592,128]{1,0:T(8,128)(2,1)} %copy-done.2, bf16[3,32,4096]{2,1,0:T(8,128)(2,1)} %gather_fusion, bf16[3,32,4096]{2,1,0:T(8,128)(2,1)} %gather_fusion.1), custom_call_target="tpu_custom_call" | custom-call | tf_op jit(solution)/shard_map/relay/pallas_call | solution.py:470
  224.6 1.3 slice_bitcast_fusion.1
  225.9 1.4 slice_bitcast_fusion
  227.3 2.7 %copy.19 = bf16[1,6,32,4096]{3,2,1,0:T(8,128)(2,1)} copy(bf16[1,6,32,4096]{3,2,1,0:T(8,128)(2,1)} %bitcast.27) | data formatting | bytes 3145728
  (5 shorter events, 0.0 us)
Async XLA Ops:
  0.6 4.2 %copy-start = (bf16[6,32,4096]{2,1,0:T(8,128)(2,1)S(1)}, bf16[6,32,4096]{2,1,0:T(8,128)(2,1)}, u32[]{:S(2)}) copy-start(bf16[6,32,4096]{2,1,0:T(8,128)(2,1)} %param.8) | copy-start | bytes 4718596
  0.6 5.7 %copy-start.1 = (bf16[6,32,4096]{2,1,0:T(8,128)(2,1)S(1)}, bf16[6,32,4096]{2,1,0:T(8,128)(2,1)}, u32[]{:S(2)}) copy-start(bf16[6,32,4096]{2,1,0:T(8,128)(2,1)} %param.7) | copy-start | bytes 4718596
  4.8 3.0 %copy-start.2 = (bf16[592,128]{1,0:T(8,128)(2,1)}, bf16[592,128]{1,0:T(8,128)(2,1)S(1)}, u32[]{:S(2)}) copy-start(bf16[592,128]{1,0:T(8,128)(2,1)S(1)} %constant_dynamic-update-slice_fusion.shard) | copy-start | bytes 454660

commit v2 on v1

--- a/solution.py
+++ b/solution.py
@@ -44,8 +44,8 @@
         self.qa = self.rp + (tiles - self.rp // 16) // 2 * 16
 
 
-def kernel(dm, shard, tok, cot, out, gout, buf, xs, ns, iv, lo, gs, dv, dl, up, dn, rr, rc, s1, t1, t2, v1, v2, s2,
-           zb, zr, yr, ss, cs, fr, fs, br, bs, os, gsm, zrr):
+def kernel(dm, order, wv, wo, ad, au, tok, cot, out, gdown, gup, shard, stage, buf, xs, nt, iv, raw, lo, gs, dv, dl,
+           up, rr, rc, s1, t1, t2, v1, v2, s2, zb, zr, yr, ss, cs, fr, fs, br, bs, os, gsm, zrr):
     nx, nz, nh, d_all, hv, hb = dm.nx, dm.nz, dm.nh, dm.d, dm.hv, dm.hb
     sec = lax.axis_index("section")
     fid = lax.axis_index("fsdp")
@@ -83,6 +83,22 @@
             src_ref=ref, dst_ref=ref, send_sem=ssem, recv_sem=ssem, device_id=d_sib, device_id_type=MESH
         ).wait_send()
 
+    @pl.when(x == 0)
+    def _():
+        pltpu.make_async_copy(tok, stage, cs.at[3]).start()
+
+    @pl.when(x == nx - 1)
+    def _():
+        pltpu.make_async_copy(cot, stage, cs.at[3]).start()
+
+    for b in range(hb):
+        shard[pl.ds(64 * b, 64)] = wv[:, 128 * b : 128 * b + 128]
+        turned = wo[128 * b : 128 * b + 128, :].astype(F32).T
+        shard[pl.ds(dm.off_out + 64 * b, 64)] = turned.astype(BF16)
+    shard[pl.ds(dm.off_down, 64)] = ad[...]
+    turned = au[...].astype(F32).T
+    shard[pl.ds(dm.off_up, 16)] = jnp.concatenate([turned, jnp.zeros_like(turned)], axis=0).astype(BF16)
+
     barrier = pltpu.get_barrier_semaphore()
 
     def greet(to):
@@ -122,6 +138,18 @@
     send(shard, own, cs.at[0], cs.at[1], d_sib)
     local = pltpu.make_async_copy(shard, own, cs.at[2])
     local.start()
+
+    @pl.when(x == 0)
+    def _():
+        pltpu.make_async_copy(tok, stage, cs.at[3]).wait()
+        for u in range(3):
+            xs[0, u] = stage[order[3 * yh + u]]
+
+    @pl.when(x == nx - 1)
+    def _():
+        pltpu.make_async_copy(cot, stage, cs.at[3]).wait()
+        for u in range(3):
+            gs[2, u] = stage[order[3 * yh + u]]
 
     def send_p(s, kind, dist_of):
         for way, (ps, to) in enumerate(((2, d_zp), (3, d_zm))):
@@ -234,18 +262,8 @@
     left(span(nz - 1, rows - qa), ss.at[10])
 
     for l in range(2):
-        raw = buf[pl.ds(l * 4 * nz, 4 * nz), pl.ds(dm.off_up, 16), :].astype(F32)
-        up[l] = raw[:, :8, :].reshape(hv, 128).astype(BF16)
-
-    @pl.when(x == 0)
-    def _():
-        for u in range(3):
-            xs[0, u] = tok[u]
-
-    @pl.when(x == nx - 1)
-    def _():
-        for u in range(3):
-            gs[2, u] = cot[u]
+        packed = buf[pl.ds(l * 4 * nz, 4 * nz), pl.ds(dm.off_up, 16), :].astype(F32)
+        up[l] = packed[:, :8, :].reshape(hv, 128).astype(BF16)
 
     tokens = dm.rows
 
@@ -271,86 +289,93 @@
         return v[:, :128] + v[:, 128:]
 
     def run_forward(u):
-        @pl.when(x > 0)
-        def _():
+        for l in range(2):
+            total = jnp.zeros((tokens, 128), F32)
+            acc = jnp.zeros((tokens, hv + 128), F32)
             for p in range(PIECES):
-                got(piece(xs, 0, u, p), fr.at[u, p])
-
-        def layer(l, carry):
-            total = jnp.zeros((tokens, 128), F32)
-            for k in range(nz):
-                v = xs[l, u, :, cols(k)].astype(F32)
-                total = total + lanes(v * v)
+                if l == 0:
+
+                    @pl.when(x > 0)
+                    def _(p=p):
+                        got(piece(xs, 0, u, p), fr.at[u, p])
+
+                for k in range(p * per_piece, (p + 1) * per_piece):
+                    v = xs[l, u, :, cols(k)]
+                    acc = acc + dot(v, w_in(l, k))
+                    v = v.astype(F32)
+                    total = total + lanes(v * v)
             inv = lax.rsqrt(jnp.sum(total, axis=-1, keepdims=True) * (1.0 / d_all) + EPS)
             iv[l, u] = jnp.broadcast_to(inv, (tokens, 128))
-            for k in range(nz):
-                ns[l, u, :, cols(k)] = (xs[l, u, :, cols(k)].astype(F32) * inv).astype(BF16)
-            acc = jnp.zeros((tokens, hv + 128), F32)
-            for k in range(nz):
-                acc = acc + dot(ns[l, u, :, cols(k)], w_in(l, k))
+            raw[l, u] = acc
+            acc = acc * inv
             low = acc[:, hv:].astype(BF16)
             lo[l, u] = low
             val = (acc[:, :hv] + dot_nt(low, up[l])).astype(BF16)
 
-            @pl.when(l + x < nx)
-            def _():
+            def outputs(l=l, val=val):
                 for p in range(PIECES):
                     for k in range(p * per_piece, (p + 1) * per_piece):
                         o = xs[l, u, :, cols(k)].astype(F32) + dot_nt(val, w_back(l, k))
                         xs[l + 1, u, :, cols(k)] = o.astype(BF16)
-                    for q in ((p - 1,) if p < PIECES - 1 else (p - 1, p)):
-                        if q >= 0:
-
-                            @pl.when(l == 1)
-                            def _(q=q):
+                    if l == 1:
+                        for q in (p - 1,) if p < PIECES - 1 else (p - 1, p):
+                            if q >= 0:
                                 send(piece(xs, 2, u, q), piece(xs, 0, u, q), fs.at[u, q], fr.at[u, q], d_xp)
 
-            return carry
-
-        lax.fori_loop(0, 2, layer, 0)
+            if l == 0:
+                outputs()
+            else:
+                pl.when(x < nx - 1)(outputs)
 
     def run_backward(u):
-        @pl.when(x < nx - 1)
-        def _():
+        for l in (1, 0):
+            acc = jnp.zeros((tokens, hv), F32)
             for p in range(PIECES):
-                got(piece(gs, 2, u, p), br.at[u, p])
-
-        def layer(i, carry):
-            l = 1 - i
-            acc = jnp.zeros((tokens, hv), F32)
-            for k in range(nz):
-                acc = acc + dot(gs[l + 1, u, :, cols(k)], w_back(l, k))
+                if l == 1:
+
+                    @pl.when(x < nx - 1)
+                    def _(p=p):
+                        got(piece(gs, 2, u, p), br.at[u, p])
+
+                for k in range(p * per_piece, (p + 1) * per_piece):
+                    acc = acc + dot(gs[l + 1, u, :, cols(k)], w_back(l, k))
             dvb = acc.astype(BF16)
             dv[l, u] = dvb
             dlb = dot(dvb, up[l]).astype(BF16)
             dl[l, u] = dlb
             both = jnp.concatenate([dvb, dlb], axis=1)
-            m = jnp.zeros((tokens, 128), F32)
-            for k in range(nz):
-                g = dot_nt(both, w_in(l, k))
-                dn[:, cols(k)] = g
-                m = m + lanes(g * xs[l, u, :, cols(k)].astype(F32))
-            mean = jnp.sum(m, axis=-1, keepdims=True) * (1.0 / d_all)
+            mean = jnp.sum(both.astype(F32) * raw[l, u], axis=-1, keepdims=True) * (1.0 / d_all)
             inv = iv[l, u][:, :1]
             scale = inv * inv * mean
             for p in range(PIECES):
                 for k in range(p * per_piece, (p + 1) * per_piece):
-                    g = dn[:, cols(k)] - xs[l, u, :, cols(k)].astype(F32) * scale
+                    g = dot_nt(both, w_in(l, k)) - xs[l, u, :, cols(k)].astype(F32) * scale
                     gs[l, u, :, cols(k)] = (gs[l + 1, u, :, cols(k)].astype(F32) + inv * g).astype(BF16)
-            for p in range(PIECES):
-
-                @pl.when((l == 0) & (x > 0))
-                def _(p=p):
-                    send(piece(gs, 0, u, p), piece(gs, 2, u, p), bs.at[u, p], br.at[u, p], d_xm)
-
-            @pl.when(l == yh)
-            def _():
+                if l == 0:
+                    for q in (p - 1,) if p < PIECES - 1 else (p - 1, p):
+                        if q >= 0:
+
+                            @pl.when(x > 0)
+                            def _(q=q):
+                                send(piece(gs, 0, u, q), piece(gs, 2, u, q), bs.at[u, q], br.at[u, q], d_xm)
+
+            @pl.when(yh == l)
+            def _(l=l):
                 pltpu.make_async_copy(gs.at[l, u], out.at[3 * yh + u], os.at[0, u]).start()
 
-            @pl.when(l != yh)
-            def _():
+            @pl.when(yh != l)
+            def _(l=l):
                 send(gs.at[l, u], out.at[3 * yh + u], os.at[1, u], os.at[2, u], d_yo)
 
+    pad = jnp.zeros((128 - 3 * tokens, 128), BF16)
+
+    def turn_normed():
+        def layer(l, carry):
+            inv = iv[l].reshape(3 * tokens, 128)[:, :1]
+            for k in range(2 * nz):
+                lane = pl.ds(128 * k, 128)
+                n_k = xs[l, :, :, lane].reshape(3 * tokens, 128).astype(F32) * inv
+                nt[l, lane, :] = jnp.concatenate([n_k.astype(BF16), pad], axis=0).T
             return carry
 
         lax.fori_loop(0, 2, layer, 0)
@@ -358,27 +383,30 @@
     last = x // (nx - 1)
 
     def turn(t, carry):
-        u = last * (t // 2) + (1 - last) * (t % 3)
-        back = last * (t % 2) + (1 - last) * (t // 3)
-
-        @pl.when(back == 0)
+        u = last * ((t // 2) % 3) + (1 - last) * (t % 4)
+        kind = last * (t % 2 + 2 * (t // 6)) + (1 - last) * (t // 4 + 2 * ((t % 4) // 3))
+
+        @pl.when(kind == 0)
         def _():
             run_forward(u)
 
-        @pl.when(back == 1)
+        @pl.when(kind == 1)
         def _():
             run_backward(u)
 
+        @pl.when(kind == 2)
+        def _():
+            turn_normed()
+
         return carry
 
-    lax.fori_loop(0, 6, turn, 0)
+    lax.fori_loop(0, 7, turn, 0)
 
     def adapter_grads(l, carry):
-        dl_all = dl[l].reshape(3 * tokens, 128)
+        dl_all = jnp.concatenate([dl[l].reshape(3 * tokens, 128), pad], axis=0)
         lo_all = lo[l].reshape(3 * tokens, 128)
         for k in range(nz):
-            n_k = ns[l, :, :, cols(k)].reshape(3 * tokens, 256)
-            g = lax.dot_general(n_k, dl_all, TN, preferred_element_type=F32).astype(BF16)
+            g = dot(nt[l, cols(k), :], dl_all).astype(BF16)
             for q in range(4):
                 rr[2 * l + q // 2, k, q % 2, pl.ds(0, 64), :] = g[64 * q : 64 * q + 64]
         dv_all = dv[l].reshape(3 * tokens, hv)
@@ -391,62 +419,70 @@
 
     lax.fori_loop(0, 2, adapter_grads, 0)
 
-    send(rr.at[:, :, 1 - c], rc, gsm.at[0], gsm.at[1], d_sib)
-    got(rc, gsm.at[1])
-
-    def add_core(i, carry):
-        a, b = i // nz, i % nz
-        s1[a, b] = (rr[a, b, c].astype(F32) + rc[a, b].astype(F32)).astype(BF16)
-        return carry
-
-    lax.fori_loop(0, 4 * nz, add_core, 0)
+    halves = ((0, 48), (48, 32))
     lo_z, hi_z = pl.ds(0, nh), pl.ds(nh, nh)
-    send(s1.at[yo, lo_z], t1, gsm.at[2], gsm.at[3], d_yp)
-    send(s1.at[yo, hi_z], t2, gsm.at[4], gsm.at[5], d_ym)
-    got(t1, gsm.at[3])
-
-    def add_near(i, carry):
-        s1[yp, i] = (s1[yp, i].astype(F32) + t1[i].astype(F32)).astype(BF16)
-        return carry
-
-    lax.fori_loop(0, nh, add_near, 0)
-    send(s1.at[yp], v1, gsm.at[6], gsm.at[7], d_yp)
-    got(t2, gsm.at[5])
-
-    def add_far(i, carry):
-        s1[ym, nh + i] = (s1[ym, nh + i].astype(F32) + t2[i].astype(F32)).astype(BF16)
-        return carry
-
-    lax.fori_loop(0, nh, add_far, 0)
-    send(s1.at[ym], v2, gsm.at[8], gsm.at[9], d_ym)
-    got(v1, gsm.at[7])
-    got(v2, gsm.at[9])
-
-    def add_y(i, carry):
-        s2[i] = (s1[y, i].astype(F32) + v1[i].astype(F32) + v2[i].astype(F32)).astype(BF16)
-        return carry
-
-    lax.fori_loop(0, nz, add_y, 0)
-
-    def z_send(i, carry):
-        zz = (z + i) % nz
-        send(s2.at[zz], zb.at[i], gsm.at[10], zrr.at[i], dev(x, y, zz, c))
-        return carry
-
-    lax.fori_loop(1, nz, z_send, 0)
-
-    def z_add(i, acc):
-        got(zb.at[i], zrr.at[i])
-        return acc + zb[i].astype(F32)
-
-    gout[...] = lax.fori_loop(1, nz, z_add, s2[z].astype(F32))
-
-    left(zb.at[pl.ds(0, nz - 1)], gsm.at[10])
-    left(rc, gsm.at[0])
-    left(t1, gsm.at[2])
-    left(t2, gsm.at[4])
-    left(v1, gsm.at[6])
-    left(v2, gsm.at[8])
+
+    def rows_of(h):
+        return pl.ds(*halves[h])
+
+    for h in range(2):
+        r = rows_of(h)
+        send(rr.at[:, :, 1 - c, r, :], rc.at[:, :, r, :], gsm.at[h, 0], gsm.at[h, 1], d_sib)
+    for h in range(2):
+        r = rows_of(h)
+        got(rc.at[:, :, r, :], gsm.at[h, 1])
+
+        def add_core(i, carry, r=r):
+            s1[i, :, r, :] = (rr[i, :, c, r, :].astype(F32) + rc[i, :, r, :].astype(F32)).astype(BF16)
+            return carry
+
+        lax.fori_loop(0, NY, add_core, 0)
+        send(s1.at[yo, lo_z, r, :], t1.at[:, r, :], gsm.at[h, 2], gsm.at[h, 3], d_yp)
+        send(s1.at[yo, hi_z, r, :], t2.at[:, r, :], gsm.at[h, 4], gsm.at[h, 5], d_ym)
+    for h in range(2):
+        r = rows_of(h)
+        got(t1.at[:, r, :], gsm.at[h, 3])
+        s1[yp, lo_z, r, :] = (s1[yp, lo_z, r, :].astype(F32) + t1[:, r, :].astype(F32)).astype(BF16)
+        got(t2.at[:, r, :], gsm.at[h, 5])
+        s1[ym, hi_z, r, :] = (s1[ym, hi_z, r, :].astype(F32) + t2[:, r, :].astype(F32)).astype(BF16)
+        send(s1.at[yp, :, r, :], v1.at[:, r, :], gsm.at[h, 6], gsm.at[h, 7], d_yp)
+        send(s1.at[ym, :, r, :], v2.at[:, r, :], gsm.at[h, 8], gsm.at[h, 9], d_ym)
+    for h in range(2):
+        r = rows_of(h)
+        got(v1.at[:, r, :], gsm.at[h, 7])
+        got(v2.at[:, r, :], gsm.at[h, 9])
+        total = s1[y, :, r, :].astype(F32) + v1[:, r, :].astype(F32) + v2[:, r, :].astype(F32)
+        s2[:, r, :] = total.astype(BF16)
+
+        def z_send(i, carry, h=h, r=r):
+            zz = (z + i) % nz
+            send(s2.at[zz, r, :], zb.at[i, r, :], gsm.at[h, 10], zrr.at[h, i], dev(x, y, zz, c))
+            return carry
+
+        lax.fori_loop(1, nz, z_send, 0)
+
+    def z_sum(h):
+        r = rows_of(h)
+
+        def z_add(i, acc):
+            got(zb.at[i, r, :], zrr.at[h, i])
+            return acc + zb[i, r, :].astype(F32)
+
+        return lax.fori_loop(1, nz, z_add, s2[z, r, :].astype(F32))
+
+    top, bottom = z_sum(0), z_sum(1)
+    gdown[pl.ds(0, 48)] = top
+    gdown[pl.ds(48, 16)] = bottom[:16]
+    gup[...] = bottom[16:24].T
+
+    for h in range(2):
+        r = rows_of(h)
+        left(zb.at[pl.ds(0, nz - 1), r, :], gsm.at[h, 10])
+        left(rc.at[:, :, r, :], gsm.at[h, 0])
+        left(t1.at[:, r, :], gsm.at[h, 2])
+        left(t2.at[:, r, :], gsm.at[h, 4])
+        left(v1.at[:, r, :], gsm.at[h, 6])
+        left(v2.at[:, r, :], gsm.at[h, 8])
     for u in range(3):
         for p in range(PIECES):
 
@@ -463,29 +499,34 @@
         got(out.at[3 * (1 - yh) + u], os.at[2, u])
 
 
-def run_all(dm, shard, tok, cot):
+def run_all(dm, order, wv, wo, ad, au, tok, cot):
     nz, d, hv, t = dm.nz, dm.d, dm.hv, dm.rows
     vm = pltpu.VMEM
     dma = pltpu.SemaphoreType.DMA
+    in_vmem = pl.BlockSpec(memory_space=vm)
+    anywhere = pl.BlockSpec(memory_space=pl.ANY)
     return pl.pallas_call(
         functools.partial(kernel, dm),
         out_shape=(
             jax.ShapeDtypeStruct((6, t, d), BF16),
-            jax.ShapeDtypeStruct((80, 128), F32),
+            jax.ShapeDtypeStruct((64, 128), F32),
+            jax.ShapeDtypeStruct((128, 8), F32),
         ),
-        in_specs=[pl.BlockSpec(memory_space=vm)] * 3,
-        out_specs=(pl.BlockSpec(memory_space=pl.ANY), pl.BlockSpec(memory_space=vm)),
+        in_specs=[pl.BlockSpec(memory_space=pltpu.SMEM)] + [in_vmem] * 4 + [anywhere] * 2,
+        out_specs=(anywhere, in_vmem, in_vmem),
         scratch_shapes=[
+            vm((dm.shard, 128), BF16),
+            vm((6, t, d), BF16),
             vm((8 * nz, dm.shard, 128), BF16),
             vm((3, 3, t, d), BF16),
-            vm((2, 3, t, d), BF16),
+            vm((2, d, 128), BF16),
             vm((2, 3, t, 128), F32),
+            vm((2, 3, t, hv + 128), F32),
             vm((2, 3, t, 128), BF16),
             vm((3, 3, t, d), BF16),
             vm((2, 3, t, hv), BF16),
             vm((2, 3, t, 128), BF16),
             vm((2, hv, 128), BF16),
-            vm((t, d), F32),
             vm((4, nz, 2, 80, 128), BF16),
             vm((4, nz, 80, 128), BF16),
             vm((4, nz, 80, 128), BF16),
@@ -498,44 +539,29 @@
             dma((2, dm.nh + 2, 4)),
             dma((nz, 4)),
             dma((12,)),
-            dma((3,)),
+            dma((4,)),
             dma((3, PIECES)),
             dma((3, PIECES)),
             dma((3, PIECES)),
             dma((3, PIECES)),
             dma((3, 3)),
-            dma((11,)),
-            dma((nz,)),
+            dma((2, 11)),
+            dma((2, nz)),
         ],
         compiler_params=pltpu.CompilerParams(
             collective_id=0, has_side_effects=True, vmem_limit_bytes=60 * 1024 * 1024
         ),
         name="relay",
-    )(shard, tok, cot)
-
-
-def lane_blocks(a):
-    return jnp.swapaxes(a.reshape(a.shape[0], -1, 128), 0, 1).reshape(-1, 128)
+    )(order, wv, wo, ad, au, tok, cot)
 
 
 def solution(mesh):
     def body(tokens, cotangent, order, w_value, w_out, adapter_down, adapter_up):
         dm = Dims(mesh, tokens.shape[1], tokens.shape[2], w_value.shape[2])
-        up_t = adapter_up[0].T
-        shard = jnp.concatenate(
-            [
-                lane_blocks(w_value[0]),
-                lane_blocks(w_out[0].T),
-                adapter_down[0],
-                up_t,
-                jnp.zeros_like(up_t),
-            ],
-            axis=0,
+        dx, down, up = run_all(
+            dm, order, w_value[0], w_out[0], adapter_down[0], adapter_up[0], tokens, cotangent
         )
-        half = lax.axis_index("section") % 2
-        mine = lax.dynamic_slice(order, (3 * half,), (3,))
-        dx, grads = run_all(dm, shard, tokens[mine], cotangent[mine])
-        return (dx[None], grads[:64][None], grads[64:72].T[None])
+        return (dx[None], down[None], up[None])
 
     return jax.shard_map(
         body,

time: 231 us -> 212 us (0.918)
  Pallas kernels: 217 us -> 200 us
  local copies, waits for them, and re-layouts: 11.6 us -> 7.82 us
    pallas_call x1, Pallas kernels: 217 us -> 200 us  [run_all(): pl.pallas_call(functools.partial(kernel, dm), out_shape=(jax.ShapeDtypeSt...]
    unnamed x11 -> x7, local copies, waits for them, and re-layouts: 4.15 us -> 7.82 us
    gather x2 -> x0, local copies, waits for them, and re-layouts: 3.03 us -> none  [body(): dx, grads = run_all(dm, shard, tokens[mine], cotangent[mine])]
    broadcast_in_dim x2 -> x0, local copies, waits for them, and re-layouts: 2.64 us -> none  [body(): return (dx[None], grads[:64][None], grads[64:72].T[None])]
where the time goes in v2:
time: 212 us; the launch traced here: 209 us
  Pallas kernels  200 us (94%)
  local copies, waits for them, and re-layouts  7.82 us (4%)
    pallas_call x1, Pallas kernels, run_all(): pl.pallas_call(functools.partial(kernel, dm), out_shape=(jax.ShapeDtypeSt...  200 us
    unnamed x7, local copies, waits for them, and re-layouts  7.82 us

profile of v2, /device:TPU:25, one launch (start us, length us, event | category | flops | bytes accessed | tf_op | source)
XLA Modules:
  0.0 208.8 jit_solution(7590261550045848435)
XLA Ops:
  0.6 1.4 copy.11
  2.0 1.6 copy.10
  3.6 200.4 %relay.1 = (bf16[6,32,4096]{2,1,0:T(8,128)(2,1)}, f32[64,128]{1,0:T(8,128)}, f32[128,8]{1,0:T(8,128)}) custom-call(s32[6]{0:T(128)} %order.1, bf16[64,512]{1,0:T(8,128)(2,1)} %bitcast.10, bf16[512,64]{1,0:T(8,128)(2,1)} %bitcast.8, bf16[64,128]{1,0:T(8,128)(2,1)} %bitcast.13, bf16[128,8]{1,0:T(8,128)(2,1)} %bitcast.9, bf16[6,32,4096]{2,1,0:T(8,128)(2,1)} %tok.1, ...), custom_call_target="tpu_custom_call" | custom-call | tf_op jit(solution)/shard_map/relay/pallas_call | solution.py:508
  204.0 1.5 copy.12
  205.5 0.0 copy-start
  205.5 2.7 %copy.15 = bf16[1,6,32,4096]{3,2,1,0:T(8,128)(2,1)} copy(bf16[1,6,32,4096]{3,2,1,0:T(8,128)(2,1)} %bitcast.7) | data formatting | bytes 3145728
  208.2 0.0 copy-done
  208.2 0.6 copy.16
Async XLA Ops:
  205.5 2.7 %copy-start = (f32[64,128]{1,0:T(8,128)S(1)}, f32[64,128]{1,0:T(8,128)}, u32[]{:S(2)}) copy-start(f32[64,128]{1,0:T(8,128)} %get-tuple-element.7) | copy-start | bytes 98308

commit v3 on v2

--- a/solution.py
+++ b/solution.py
@@ -44,7 +44,7 @@
         self.qa = self.rp + (tiles - self.rp // 16) // 2 * 16
 
 
-def kernel(dm, order, wv, wo, ad, au, tok, cot, out, gdown, gup, shard, stage, buf, xs, nt, iv, raw, lo, gs, dv, dl,
+def kernel(dm, order, wv, wo, ad, au, tok, cot, out, gdown, gup, shard, stage, buf, xs, nt, iv, raw, pre, lo, gs, dv, dl,
            up, rr, rc, s1, t1, t2, v1, v2, s2, zb, zr, yr, ss, cs, fr, fs, br, bs, os, gsm, zrr):
     nx, nz, nh, d_all, hv, hb = dm.nx, dm.nz, dm.nh, dm.d, dm.hv, dm.hb
     sec = lax.axis_index("section")
@@ -93,10 +93,9 @@
 
     for b in range(hb):
         shard[pl.ds(64 * b, 64)] = wv[:, 128 * b : 128 * b + 128]
-        turned = wo[128 * b : 128 * b + 128, :].astype(F32).T
-        shard[pl.ds(dm.off_out + 64 * b, 64)] = turned.astype(BF16)
+        shard[pl.ds(dm.off_out + 64 * b, 64)] = wo[:, 128 * b : 128 * b + 128]
     shard[pl.ds(dm.off_down, 64)] = ad[...]
-    turned = au[...].astype(F32).T
+    turned = au[...].astype(F32)
     shard[pl.ds(dm.off_up, 16)] = jnp.concatenate([turned, jnp.zeros_like(turned)], axis=0).astype(BF16)
 
     barrier = pltpu.get_barrier_semaphore()
@@ -104,18 +103,11 @@
     def greet(to):
         pl.semaphore_signal(barrier, inc=1, device_id=to, device_id_type=MESH)
 
-    for to in (d_sib, d_yp, d_ym, d_yo):
+    d_xs = dev((x + nx - 1) % nx, y, z, c), dev((x + 1) % nx, y, z, c)
+    peers = (d_sib, d_yp, d_ym, d_zp, d_zm, *d_xs)
+    for to in peers:
         greet(to)
-
-    def greet_z(i, _):
-        greet(dev(x, y, (z + i) % nz, c))
-        return _
-
-    lax.fori_loop(1, nz, greet_z, 0)
-
-    greet(dev((x + nx - 1) % nx, y, z, c))
-    greet(dev((x + 1) % nx, y, z, c))
-    pl.semaphore_wait(barrier, 4 + nz - 1 + 2)
+    pl.semaphore_wait(barrier, len(peers))
 
     rows, rp, half, qa = dm.shard, dm.rp, dm.half, dm.qa
 
@@ -131,8 +123,7 @@
     me = slot(y, z, c)
     own = buf.at[me]
     send(shard, own, ss.at[0], zr.at[0, 1, 0], d_zp)
-    if nh > 1:
-        send(shard, own, ss.at[1], zr.at[1, 1, 0], d_zm)
+    send(shard, own, ss.at[1], zr.at[1, 1, 0], d_zm)
     send(shard, own, ss.at[4], yr.at[0, 0], d_yp)
     send(shard, own, ss.at[11], yr.at[0, 1], d_ym)
     send(shard, own, cs.at[0], cs.at[1], d_sib)
@@ -153,8 +144,7 @@
 
     def send_p(s, kind, dist_of):
         for way, (ps, to) in enumerate(((2, d_zp), (3, d_zm))):
-            if way == 0 or nh > 1:
-                move(s, 0, rp, ss.at[ps], zr.at[way, dist_of, kind], to)
+            move(s, 0, rp, ss.at[ps], zr.at[way, dist_of, kind], to)
 
     s_m, s_p, s_o = slot(ym, z, c), slot(yp, z, c), slot(yo, z, c)
     got(part(s_m, 0, rows), yr.at[0, 0])
@@ -175,6 +165,9 @@
     def limit(way):
         return nh if way == 0 else nh - 1
 
+    def limit_p(way):
+        return nh - 1 if way == 0 else nh
+
     def z_shard(way, d):
         s = slot(y, z_from(way, d), c)
         e = e_of(way, d)
@@ -193,7 +186,7 @@
             s = slot(col, z_from(way, d), c)
             got(part(s, 0, rp), zr.at[way, d, kind])
 
-            @pl.when(d < limit(way))
+            @pl.when(d < limit_p(way))
             def _(s=s, kind=kind):
                 move(s, 0, rp, ss.at[2 + way], zr.at[way, d + 1, kind], (d_zp, d_zm)[way])
 
@@ -230,7 +223,7 @@
             to_sib(s_o, half, rows)
 
         for way in (0, 1):
-            pl.when(d <= limit(way))(functools.partial(z_parts, way, d))
+            pl.when(d <= limit_p(way))(functools.partial(z_parts, way, d))
         for way in (0, 1):
             pl.when((d > 1) & (d <= limit(way) + 1))(functools.partial(y_near, way, d - 1))
         for way in (0, 1):
@@ -248,10 +241,9 @@
         return buf.at[pl.ds(0, n), pl.ds(0, r), :]
 
     left(span(nh, rows), ss.at[0])
-    left(span(3 * nh, rp), ss.at[2])
-    if nh > 1:
-        left(span(nh - 1, rows), ss.at[1])
-        left(span(3 * (nh - 1), rp), ss.at[3])
+    left(span(nh - 1, rows), ss.at[1])
+    left(span(3 * (nh - 1), rp), ss.at[2])
+    left(span(3 * nh, rp), ss.at[3])
     left(span(1, rows), ss.at[4])
     left(span(1, rows), ss.at[11])
     left(span(1, half), ss.at[5])
@@ -327,45 +319,77 @@
             else:
                 pl.when(x < nx - 1)(outputs)
 
+    def adapter_side(l, u, acc):
+        dvb = acc.astype(BF16)
+        dv[l, u] = dvb
+        dlb = dot(dvb, up[l]).astype(BF16)
+        dl[l, u] = dlb
+        return jnp.concatenate([dvb, dlb], axis=1)
+
+    def ahead(u, carry):
+        acc = jnp.zeros((tokens, hv), F32)
+        for k in range(nz):
+            acc = acc + dot(gs[2, u, :, cols(k)], w_back(1, k))
+        both = adapter_side(1, u, acc)
+        for k in range(nz):
+            pre[u, :, cols(k)] = dot_nt(both, w_in(1, k))
+        return carry
+
+    @pl.when(x == nx - 1)
+    def _():
+        lax.fori_loop(0, 3, ahead, 0)
+
+    def input_grad(l, u, both, product, after):
+        mean = jnp.sum(both.astype(F32) * raw[l, u], axis=-1, keepdims=True) * (1.0 / d_all)
+        inv = iv[l, u][:, :1]
+        scale = inv * inv * mean
+        for p in range(PIECES):
+            for k in range(p * per_piece, (p + 1) * per_piece):
+                g = product(k) - xs[l, u, :, cols(k)].astype(F32) * scale
+                gs[l, u, :, cols(k)] = (gs[l + 1, u, :, cols(k)].astype(F32) + inv * g).astype(BF16)
+            after(p)
+
+    def hand_out(l, u):
+        @pl.when(yh == l)
+        def _():
+            pltpu.make_async_copy(gs.at[l, u], out.at[3 * yh + u], os.at[0, u]).start()
+
+        @pl.when(yh != l)
+        def _():
+            send(gs.at[l, u], out.at[3 * yh + u], os.at[1, u], os.at[2, u], d_yo)
+
     def run_backward(u):
-        for l in (1, 0):
+        @pl.when(x == nx - 1)
+        def _():
+            both = jnp.concatenate([dv[1, u], dl[1, u]], axis=1)
+            input_grad(1, u, both, lambda k: pre[u, :, cols(k)], lambda p: None)
+
+        @pl.when(x < nx - 1)
+        def _():
             acc = jnp.zeros((tokens, hv), F32)
             for p in range(PIECES):
-                if l == 1:
-
-                    @pl.when(x < nx - 1)
-                    def _(p=p):
-                        got(piece(gs, 2, u, p), br.at[u, p])
-
+                got(piece(gs, 2, u, p), br.at[u, p])
                 for k in range(p * per_piece, (p + 1) * per_piece):
-                    acc = acc + dot(gs[l + 1, u, :, cols(k)], w_back(l, k))
-            dvb = acc.astype(BF16)
-            dv[l, u] = dvb
-            dlb = dot(dvb, up[l]).astype(BF16)
-            dl[l, u] = dlb
-            both = jnp.concatenate([dvb, dlb], axis=1)
-            mean = jnp.sum(both.astype(F32) * raw[l, u], axis=-1, keepdims=True) * (1.0 / d_all)
-            inv = iv[l, u][:, :1]
-            scale = inv * inv * mean
-            for p in range(PIECES):
-                for k in range(p * per_piece, (p + 1) * per_piece):
-                    g = dot_nt(both, w_in(l, k)) - xs[l, u, :, cols(k)].astype(F32) * scale
-                    gs[l, u, :, cols(k)] = (gs[l + 1, u, :, cols(k)].astype(F32) + inv * g).astype(BF16)
-                if l == 0:
-                    for q in (p - 1,) if p < PIECES - 1 else (p - 1, p):
-                        if q >= 0:
-
-                            @pl.when(x > 0)
-                            def _(q=q):
-                                send(piece(gs, 0, u, q), piece(gs, 2, u, q), bs.at[u, q], br.at[u, q], d_xm)
-
-            @pl.when(yh == l)
-            def _(l=l):
-                pltpu.make_async_copy(gs.at[l, u], out.at[3 * yh + u], os.at[0, u]).start()
-
-            @pl.when(yh != l)
-            def _(l=l):
-                send(gs.at[l, u], out.at[3 * yh + u], os.at[1, u], os.at[2, u], d_yo)
+                    acc = acc + dot(gs[2, u, :, cols(k)], w_back(1, k))
+            both = adapter_side(1, u, acc)
+            input_grad(1, u, both, lambda k: dot_nt(both, w_in(1, k)), lambda p: None)
+
+        hand_out(1, u)
+        acc = jnp.zeros((tokens, hv), F32)
+        for k in range(nz):
+            acc = acc + dot(gs[1, u, :, cols(k)], w_back(0, k))
+        both = adapter_side(0, u, acc)
+
+        def after(p):
+            for q in (p - 1,) if p < PIECES - 1 else (p - 1, p):
+                if q >= 0:
+
+                    @pl.when(x > 0)
+                    def _(q=q):
+                        send(piece(gs, 0, u, q), piece(gs, 2, u, q), bs.at[u, q], br.at[u, q], d_xm)
+
+        input_grad(0, u, both, lambda k: dot_nt(both, w_in(0, k)), after)
+        hand_out(0, u)
 
     pad = jnp.zeros((128 - 3 * tokens, 128), BF16)
 
@@ -473,7 +497,7 @@
     top, bottom = z_sum(0), z_sum(1)
     gdown[pl.ds(0, 48)] = top
     gdown[pl.ds(48, 16)] = bottom[:16]
-    gup[...] = bottom[16:24].T
+    gup[...] = bottom[16:24]
 
     for h in range(2):
         r = rows_of(h)
@@ -510,7 +534,7 @@
         out_shape=(
             jax.ShapeDtypeStruct((6, t, d), BF16),
             jax.ShapeDtypeStruct((64, 128), F32),
-            jax.ShapeDtypeStruct((128, 8), F32),
+            jax.ShapeDtypeStruct((8, 128), F32),
         ),
         in_specs=[pl.BlockSpec(memory_space=pltpu.SMEM)] + [in_vmem] * 4 + [anywhere] * 2,
         out_specs=(anywhere, in_vmem, in_vmem),
@@ -522,6 +546,7 @@
             vm((2, d, 128), BF16),
             vm((2, 3, t, 128), F32),
             vm((2, 3, t, hv + 128), F32),
+            vm((3, t, d), F32),
             vm((2, 3, t, 128), BF16),
             vm((3, 3, t, d), BF16),
             vm((2, 3, t, hv), BF16),
@@ -549,7 +574,7 @@
             dma((2, nz)),
         ],
         compiler_params=pltpu.CompilerParams(
-            collective_id=0, has_side_effects=True, vmem_limit_bytes=60 * 1024 * 1024
+            collective_id=0, has_side_effects=True, vmem_limit_bytes=44 * 1024 * 1024
         ),
         name="relay",
     )(order, wv, wo, ad, au, tok, cot)
@@ -559,9 +584,9 @@
     def body(tokens, cotangent, order, w_value, w_out, adapter_down, adapter_up):
         dm = Dims(mesh, tokens.shape[1], tokens.shape[2], w_value.shape[2])
         dx, down, up = run_all(
-            dm, order, w_value[0], w_out[0], adapter_down[0], adapter_up[0], tokens, cotangent
+            dm, order, w_value[0], w_out[0].T, adapter_down[0], adapter_up[0].T, tokens, cotangent
         )
-        return (dx[None], down[None], up[None])
+        return (dx[None], down[None], up.T[None])
 
     return jax.shard_map(
         body,

time: 212 us -> 201 us (0.948)
  Pallas kernels: 200 us -> 188 us
    pallas_call x1, Pallas kernels: 200 us -> 188 us  [run_all(): pl.pallas_call(functools.partial(kernel, dm), out_shape=(jax.ShapeDtypeSt...]
    unnamed x7 -> x17, local copies, waits for them, and re-layouts: 7.82 us -> 8.89 us
where the time goes in v3:
time: 201 us; the launch traced here: 197 us
  Pallas kernels  188 us (94%)
  local copies, waits for them, and re-layouts  8.89 us (4%)
    pallas_call x1, Pallas kernels, run_all(): pl.pallas_call(functools.partial(kernel, dm), out_shape=(jax.ShapeDtypeSt...  188 us
    unnamed x17, local copies, waits for them, and re-layouts  8.89 us

profile of v3, /device:TPU:25, one launch (start us, length us, event | category | flops | bytes accessed | tf_op | source)
XLA Modules:
  0.0 197.2 jit_solution(9159026964028550225)
XLA Ops:
  0.6 0.0 copy-start
  0.6 1.4 copy-done
  2.0 0.0 copy-start.1
  2.0 1.4 copy-done.1
  3.5 0.0 copy-start.2
  3.5 0.8 copy-done.2
  4.3 0.0 copy-start.3
  4.3 0.8 copy-done.3
  5.1 0.0 copy-start.4
  5.1 0.7 copy-done.4
  5.8 0.0 copy-start.5
  5.8 0.7 copy-done.5
  6.5 0.0 copy-start.6
  6.5 0.7 copy-done.6
  7.2 187.6 %relay.1 = (bf16[6,32,4096]{2,1,0:T(8,128)(2,1)S(1)}, f32[64,128]{1,0:T(8,128)S(1)}, f32[8,128]{1,0:T(8,128)S(1)}) custom-call(s32[6]{0:T(128)S(1)} %copy-done.6, bf16[64,512]{1,0:T(8,128)(2,1)S(1)} %bitcast.14, bf16[64,512]{1,0:T(8,128)(2,1)S(1)} %bitcast.15, bf16[64,128]{1,0:T(8,128)(2,1)S(1)} %bitcast.17, bf16[8,128]{1,0:T(8,128)(2,1)S(1)} %bitcast.19, ...), custom_call_target="tpu_custom_call" | custom-call | tf_op jit(solution)/shard_map/relay/pallas_call | solution.py:532
  194.8 1.1 copy.13
  195.9 0.6 copy.14
  196.6 0.6 copy.15
Async XLA Ops:
  0.6 1.4 copy-start
  2.0 1.4 copy-start.1
  3.5 0.8 copy-start.2
  4.3 0.8 copy-start.3
  5.1 0.7 copy-start.4
  5.8 0.7 copy-start.5
  6.5 0.7 copy-start.6

commit v4 on v3

--- a/solution.py
+++ b/solution.py
@@ -44,8 +44,8 @@
         self.qa = self.rp + (tiles - self.rp // 16) // 2 * 16
 
 
-def kernel(dm, order, wv, wo, ad, au, tok, cot, out, gdown, gup, shard, stage, buf, xs, nt, iv, raw, pre, lo, gs, dv, dl,
-           up, rr, rc, s1, t1, t2, v1, v2, s2, zb, zr, yr, ss, cs, fr, fs, br, bs, os, gsm, zrr):
+def kernel(dm, order, wv_in, wo_in, ad_in, au_in, tok, cot, out, gdown, gup, wv, wo, ad, au, shard, stage, buf, xs, nt, iv, raw, pre, lo, gs, dv, dl,
+           up, rr, rc, s1, t1, t2, v1, v2, s2, zb, ins, zr, yr, ss, cs, fr, fs, br, bs, os, gsm, zrr):
     nx, nz, nh, d_all, hv, hb = dm.nx, dm.nz, dm.nh, dm.d, dm.hv, dm.hb
     sec = lax.axis_index("section")
     fid = lax.axis_index("fsdp")
@@ -83,6 +83,22 @@
             src_ref=ref, dst_ref=ref, send_sem=ssem, recv_sem=ssem, device_id=d_sib, device_id_type=MESH
         ).wait_send()
 
+    barrier = pltpu.get_barrier_semaphore()
+
+    def greet(to):
+        pl.semaphore_signal(barrier, inc=1, device_id=to, device_id_type=MESH)
+
+    d_xs = dev((x + nx - 1) % nx, y, z, c), dev((x + 1) % nx, y, z, c)
+    peers = (d_sib, d_yp, d_ym, d_zp, d_zm, *d_xs)
+    for to in peers:
+        greet(to)
+    fetches = [
+        pltpu.make_async_copy(src, dst, ins.at[i])
+        for i, (src, dst) in enumerate(((wv_in, wv), (wo_in, wo), (ad_in, ad), (au_in, au)))
+    ]
+    for f in fetches:
+        f.start()
+
     @pl.when(x == 0)
     def _():
         pltpu.make_async_copy(tok, stage, cs.at[3]).start()
@@ -91,6 +107,8 @@
     def _():
         pltpu.make_async_copy(cot, stage, cs.at[3]).start()
 
+    for f in fetches:
+        f.wait()
     for b in range(hb):
         shard[pl.ds(64 * b, 64)] = wv[:, 128 * b : 128 * b + 128]
         shard[pl.ds(dm.off_out + 64 * b, 64)] = wo[:, 128 * b : 128 * b + 128]
@@ -98,15 +116,6 @@
     turned = au[...].astype(F32)
     shard[pl.ds(dm.off_up, 16)] = jnp.concatenate([turned, jnp.zeros_like(turned)], axis=0).astype(BF16)
 
-    barrier = pltpu.get_barrier_semaphore()
-
-    def greet(to):
-        pl.semaphore_signal(barrier, inc=1, device_id=to, device_id_type=MESH)
-
-    d_xs = dev((x + nx - 1) % nx, y, z, c), dev((x + 1) % nx, y, z, c)
-    peers = (d_sib, d_yp, d_ym, d_zp, d_zm, *d_xs)
-    for to in peers:
-        greet(to)
     pl.semaphore_wait(barrier, len(peers))
 
     rows, rp, half, qa = dm.shard, dm.rp, dm.half, dm.qa
@@ -235,23 +244,6 @@
     local.wait()
     half_all = buf.at[pl.ds(0, 4 * nz)]
     got(half_all, cs.at[1])
-    left(half_all, cs.at[0])
-
-    def span(n, r):
-        return buf.at[pl.ds(0, n), pl.ds(0, r), :]
-
-    left(span(nh, rows), ss.at[0])
-    left(span(nh - 1, rows), ss.at[1])
-    left(span(3 * (nh - 1), rp), ss.at[2])
-    left(span(3 * nh, rp), ss.at[3])
-    left(span(1, rows), ss.at[4])
-    left(span(1, rows), ss.at[11])
-    left(span(1, half), ss.at[5])
-    left(span(1, rows - half), ss.at[6])
-    left(span(nz - 1, rows - rp), ss.at[7])
-    left(span(nz - 1, rows - rp), ss.at[8])
-    left(span(nz - 1, qa - rp), ss.at[9])
-    left(span(nz - 1, rows - qa), ss.at[10])
 
     for l in range(2):
         packed = buf[pl.ds(l * 4 * nz, 4 * nz), pl.ds(dm.off_up, 16), :].astype(F32)
@@ -426,7 +418,7 @@
 
     lax.fori_loop(0, 7, turn, 0)
 
-    def adapter_grads(l, carry):
+    def adapter_grads(l):
         dl_all = jnp.concatenate([dl[l].reshape(3 * tokens, 128), pad], axis=0)
         lo_all = lo[l].reshape(3 * tokens, 128)
         for k in range(nz):
@@ -439,9 +431,11 @@
             g_q = g[:, q]
             padded = jnp.concatenate([g_q, jnp.zeros_like(g_q)], axis=1).astype(BF16)
             rr[2 * l + q // 2, :, q % 2, pl.ds(64, 16), :] = padded
-        return carry
-
-    lax.fori_loop(0, 2, adapter_grads, 0)
+
+    for l in range(2):
+        adapter_grads(l)
+        two = pl.ds(2 * l, 2)
+        send(rr.at[two, :, 1 - c], rc.at[two], gsm.at[l, 0], gsm.at[l, 1], d_sib)
 
     halves = ((0, 48), (48, 32))
     lo_z, hi_z = pl.ds(0, nh), pl.ds(nh, nh)
@@ -449,12 +443,10 @@
     def rows_of(h):
         return pl.ds(*halves[h])
 
+    for l in range(2):
+        got(rc.at[pl.ds(2 * l, 2)], gsm.at[l, 1])
     for h in range(2):
         r = rows_of(h)
-        send(rr.at[:, :, 1 - c, r, :], rc.at[:, :, r, :], gsm.at[h, 0], gsm.at[h, 1], d_sib)
-    for h in range(2):
-        r = rows_of(h)
-        got(rc.at[:, :, r, :], gsm.at[h, 1])
 
         def add_core(i, carry, r=r):
             s1[i, :, r, :] = (rr[i, :, c, r, :].astype(F32) + rc[i, :, r, :].astype(F32)).astype(BF16)
@@ -478,12 +470,20 @@
         total = s1[y, :, r, :].astype(F32) + v1[:, r, :].astype(F32) + v2[:, r, :].astype(F32)
         s2[:, r, :] = total.astype(BF16)
 
-        def z_send(i, carry, h=h, r=r):
-            zz = (z + i) % nz
-            send(s2.at[zz, r, :], zb.at[i, r, :], gsm.at[h, 10], zrr.at[h, i], dev(x, y, zz, c))
+        def z_send(j, carry, h=h, r=r):
+            def to(i):
+                zz = (z + i) % nz
+                send(s2.at[zz, r, :], zb.at[i, r, :], gsm.at[h, 10], zrr.at[h, i], dev(x, y, zz, c))
+
+            to(nh - j)
+
+            @pl.when(j > 0)
+            def _():
+                to(nh + j)
+
             return carry
 
-        lax.fori_loop(1, nz, z_send, 0)
+        lax.fori_loop(0, nh, z_send, 0)
 
     def z_sum(h):
         r = rows_of(h)
@@ -499,10 +499,27 @@
     gdown[pl.ds(48, 16)] = bottom[:16]
     gup[...] = bottom[16:24]
 
+    left(half_all, cs.at[0])
+
+    def span(n, r):
+        return buf.at[pl.ds(0, n), pl.ds(0, r), :]
+
+    left(span(nh, rows), ss.at[0])
+    left(span(nh - 1, rows), ss.at[1])
+    left(span(3 * (nh - 1), rp), ss.at[2])
+    left(span(3 * nh, rp), ss.at[3])
+    left(span(1, rows), ss.at[4])
+    left(span(1, rows), ss.at[11])
+    left(span(1, half), ss.at[5])
+    left(span(1, rows - half), ss.at[6])
+    left(span(nz - 1, rows - rp), ss.at[7])
+    left(span(nz - 1, rows - rp), ss.at[8])
+    left(span(nz - 1, qa - rp), ss.at[9])
+    left(span(nz - 1, rows - qa), ss.at[10])
     for h in range(2):
         r = rows_of(h)
         left(zb.at[pl.ds(0, nz - 1), r, :], gsm.at[h, 10])
-        left(rc.at[:, :, r, :], gsm.at[h, 0])
+        left(rc.at[pl.ds(2 * h, 2)], gsm.at[h, 0])
         left(t1.at[:, r, :], gsm.at[h, 2])
         left(t2.at[:, r, :], gsm.at[h, 4])
         left(v1.at[:, r, :], gsm.at[h, 6])
@@ -529,6 +546,7 @@
     dma = pltpu.SemaphoreType.DMA
     in_vmem = pl.BlockSpec(memory_space=vm)
     anywhere = pl.BlockSpec(memory_space=pl.ANY)
+    in_hbm = pl.BlockSpec(memory_space=pltpu.HBM)
     return pl.pallas_call(
         functools.partial(kernel, dm),
         out_shape=(
@@ -536,9 +554,10 @@
             jax.ShapeDtypeStruct((64, 128), F32),
             jax.ShapeDtypeStruct((8, 128), F32),
         ),
-        in_specs=[pl.BlockSpec(memory_space=pltpu.SMEM)] + [in_vmem] * 4 + [anywhere] * 2,
+        in_specs=[pl.BlockSpec(memory_space=pltpu.SMEM)] + [in_hbm] * 6,
         out_specs=(anywhere, in_vmem, in_vmem),
         scratch_shapes=[
+            *(vm(a.shape, BF16) for a in (wv, wo, ad, au)),
             vm((dm.shard, 128), BF16),
             vm((6, t, d), BF16),
             vm((8 * nz, dm.shard, 128), BF16),
@@ -561,6 +580,7 @@
             vm((nz, 80, 128), BF16),
             vm((nz, 80, 128), BF16),
             vm((nz, 80, 128), BF16),
+            dma((4,)),
             dma((2, dm.nh + 2, 4)),
             dma((nz, 4)),
             dma((12,)),
@@ -574,7 +594,7 @@
             dma((2, nz)),
         ],
         compiler_params=pltpu.CompilerParams(
-            collective_id=0, has_side_effects=True, vmem_limit_bytes=44 * 1024 * 1024
+            collective_id=0, has_side_effects=True, vmem_limit_bytes=62 * 1024 * 1024
         ),
         name="relay",
     )(order, wv, wo, ad, au, tok, cot)

time: 201 us -> 201 us (level)
  Pallas kernels: 188 us -> 194 us
  local copies, waits for them, and re-layouts: 8.89 us -> 3.92 us
    pallas_call x1, Pallas kernels: 188 us -> 194 us  [run_all(): pl.pallas_call(functools.partial(kernel, dm), out_shape=(jax.ShapeDtypeSt...]
    unnamed x17 -> x7, local copies, waits for them, and re-layouts: 8.89 us -> 3.92 us
where the time goes in v4:
time: 201 us; the launch traced here: 199 us
  Pallas kernels  194 us (97%)
  local copies, waits for them, and re-layouts  3.92 us (2%)
    pallas_call x1, Pallas kernels, run_all(): pl.pallas_call(functools.partial(kernel, dm), out_shape=(jax.ShapeDtypeSt...  194 us

profile of v4, /device:TPU:25, one launch (start us, length us, event | category | flops | bytes accessed | tf_op | source)
XLA Modules:
  0.0 199.0 jit_solution(897149042570963017)
XLA Ops:
  0.6 194.5 %relay.1 = (bf16[6,32,4096]{2,1,0:T(8,128)(2,1)}, f32[64,128]{1,0:T(8,128)}, f32[8,128]{1,0:T(8,128)}) custom-call(s32[6]{0:T(128)} %order.1, bf16[64,512]{1,0:T(8,128)(2,1)} %bitcast.14, bf16[64,512]{1,0:T(8,128)(2,1)} %bitcast.15, bf16[64,128]{1,0:T(8,128)(2,1)} %bitcast.17, bf16[8,128]{1,0:T(8,128)(2,1)} %bitcast.19, bf16[6,32,4096]{2,1,0:T(8,128)(2,1)} %tok.1, ...), custom_call_target="tpu_custom_call" | custom-call | tf_op jit(solution)/shard_map/relay/pallas_call | solution.py:550
  195.1 0.0 copy-start
  195.1 0.0 copy-start.1
  195.1 2.7 %copy.13 = bf16[1,6,32,4096]{3,2,1,0:T(8,128)(2,1)} copy(bf16[1,6,32,4096]{3,2,1,0:T(8,128)(2,1)} %bitcast.13) | data formatting | bytes 3145728
  197.8 0.0 copy-done
  197.8 0.6 copy.14
  198.4 0.0 copy-done.1
  198.4 0.6 copy.15
Async XLA Ops:
  195.1 2.7 %copy-start = (f32[64,128]{1,0:T(8,128)S(1)}, f32[64,128]{1,0:T(8,128)}, u32[]{:S(2)}) copy-start(f32[64,128]{1,0:T(8,128)} %get-tuple-element.7) | copy-start | bytes 98308
  195.1 3.3 %copy-start.1 = (f32[8,128]{1,0:T(8,128)S(1)}, f32[8,128]{1,0:T(8,128)}, u32[]{:S(2)}) copy-start(f32[8,128]{1,0:T(8,128)} %get-tuple-element.8) | copy-start | bytes 12292

commit v5 on v4

--- a/solution.py
+++ b/solution.py
@@ -45,7 +45,7 @@
 
 
 def kernel(dm, order, wv_in, wo_in, ad_in, au_in, tok, cot, out, gdown, gup, wv, wo, ad, au, shard, stage, buf, xs, nt, iv, raw, pre, lo, gs, dv, dl,
-           up, rr, rc, s1, t1, t2, v1, v2, s2, zb, ins, zr, yr, ss, cs, fr, fs, br, bs, os, gsm, zrr):
+           up, rr, rc, s1, t1, t2, v1, v2, s2, zb, zs, zf, ins, zr, yr, ss, cs, fr, fs, br, bs, os, gsm, zrr):
     nx, nz, nh, d_all, hv, hb = dm.nx, dm.nz, dm.nh, dm.d, dm.hv, dm.hb
     sec = lax.axis_index("section")
     fid = lax.axis_index("fsdp")
@@ -438,6 +438,14 @@
         send(rr.at[two, :, 1 - c], rc.at[two], gsm.at[l, 0], gsm.at[l, 1], d_sib)
 
     halves = ((0, 48), (48, 32))
+    steps = (nh - 2) // 2
+
+    def at(way, dist):
+        return (z + dist) % nz if way == 0 else (z + nz - dist) % nz
+
+    def z_move(src, dst, h, way, j, dist):
+        send(src, dst, zrr.at[0, h, way, j], zrr.at[1, h, way, j], dev(x, y, at(way, dist), c))
+
     lo_z, hi_z = pl.ds(0, nh), pl.ds(nh, nh)
 
     def rows_of(h):
@@ -470,29 +478,33 @@
         total = s1[y, :, r, :].astype(F32) + v1[:, r, :].astype(F32) + v2[:, r, :].astype(F32)
         s2[:, r, :] = total.astype(BF16)
 
-        def z_send(j, carry, h=h, r=r):
-            def to(i):
-                zz = (z + i) % nz
-                send(s2.at[zz, r, :], zb.at[i, r, :], gsm.at[h, 10], zrr.at[h, i], dev(x, y, zz, c))
-
-            to(nh - j)
-
-            @pl.when(j > 0)
-            def _():
-                to(nh + j)
-
-            return carry
-
-        lax.fori_loop(0, nh, z_send, 0)
+        for way in (0, 1):
+            zs[way, 0, r, :] = s2[at(way, nh - 1), r, :]
+            zs[way, 1, r, :] = s2[at(way, nh), r, :] if way == 0 else jnp.zeros((halves[h][1], 128), BF16)
+            z_move(zs.at[way, :, r, :], zb.at[way, 0, :, r, :], h, way, 0, 2)
+
+    for j in range(steps):
+        for h in range(2):
+            r = rows_of(h)
+            for way in (0, 1):
+                got(zb.at[way, j, :, r, :], zrr.at[1, h, way, j])
+                for i in range(2):
+                    mine = s2[at(way, nh - 3 - 2 * j + i), r, :].astype(F32)
+                    zb[way, j, i, r, :] = (zb[way, j, i, r, :].astype(F32) + mine).astype(BF16)
+                if j < steps - 1:
+                    z_move(zb.at[way, j, :, r, :], zb.at[way, j + 1, :, r, :], h, way, j + 1, 2)
+                else:
+                    for i in range(2):
+                        z_move(zb.at[way, j, i, r, :], zf.at[way, i, r, :], h, way, steps + i, i + 1)
 
     def z_sum(h):
         r = rows_of(h)
-
-        def z_add(i, acc):
-            got(zb.at[i, r, :], zrr.at[h, i])
-            return acc + zb[i, r, :].astype(F32)
-
-        return lax.fori_loop(1, nz, z_add, s2[z, r, :].astype(F32))
+        acc = s2[z, r, :].astype(F32)
+        for way in (0, 1):
+            for i in range(2):
+                got(zf.at[way, i, r, :], zrr.at[1, h, way, steps + i])
+                acc = acc + zf[way, i, r, :].astype(F32)
+        return acc
 
     top, bottom = z_sum(0), z_sum(1)
     gdown[pl.ds(0, 48)] = top
@@ -518,7 +530,11 @@
     left(span(nz - 1, rows - qa), ss.at[10])
     for h in range(2):
         r = rows_of(h)
-        left(zb.at[pl.ds(0, nz - 1), r, :], gsm.at[h, 10])
+        for way in (0, 1):
+            for j in range(steps):
+                left(zs.at[way, :, r, :], zrr.at[0, h, way, j])
+            for i in range(2):
+                left(zf.at[way, i, r, :], zrr.at[0, h, way, steps + i])
         left(rc.at[pl.ds(2 * h, 2)], gsm.at[h, 0])
         left(t1.at[:, r, :], gsm.at[h, 2])
         left(t2.at[:, r, :], gsm.at[h, 4])
@@ -579,7 +595,9 @@
             vm((nz, 80, 128), BF16),
             vm((nz, 80, 128), BF16),
             vm((nz, 80, 128), BF16),
-            vm((nz, 80, 128), BF16),
+            vm((2, dm.nh // 2 - 1, 2, 80, 128), BF16),
+            vm((2, 2, 80, 128), BF16),
+            vm((2, 2, 80, 128), BF16),
             dma((4,)),
             dma((2, dm.nh + 2, 4)),
             dma((nz, 4)),
@@ -591,7 +609,7 @@
             dma((3, PIECES)),
             dma((3, 3)),
             dma((2, 11)),
-            dma((2, nz)),
+            dma((2, 2, 2, dm.nh // 2 + 1)),
         ],
         compiler_params=pltpu.CompilerParams(
             collective_id=0, has_side_effects=True, vmem_limit_bytes=62 * 1024 * 1024

time: 201 us -> 200 us (level)
    pallas_call x1, Pallas kernels: 194 us -> 192 us  [run_all(): pl.pallas_call(functools.partial(kernel, dm), out_shape=(jax.ShapeDtypeSt...]
where the time goes in v5:
time: 200 us; the launch traced here: 197 us
  Pallas kernels  192 us (96%)
  local copies, waits for them, and re-layouts  3.92 us (2%)
    pallas_call x1, Pallas kernels, run_all(): pl.pallas_call(functools.partial(kernel, dm), out_shape=(jax.ShapeDtypeSt...  192 us

profile of v5, /device:TPU:25, one launch (start us, length us, event | category | flops | bytes accessed | tf_op | source)
XLA Modules:
  0.0 196.7 jit_solution(8836631845907780875)
XLA Ops:
  0.6 192.1 %relay.1 = (bf16[6,32,4096]{2,1,0:T(8,128)(2,1)}, f32[64,128]{1,0:T(8,128)}, f32[8,128]{1,0:T(8,128)}) custom-call(s32[6]{0:T(128)} %order.1, bf16[64,512]{1,0:T(8,128)(2,1)} %bitcast.14, bf16[64,512]{1,0:T(8,128)(2,1)} %bitcast.15, bf16[64,128]{1,0:T(8,128)(2,1)} %bitcast.17, bf16[8,128]{1,0:T(8,128)(2,1)} %bitcast.19, bf16[6,32,4096]{2,1,0:T(8,128)(2,1)} %tok.1, ...), custom_call_target="tpu_custom_call" | custom-call | tf_op jit(solution)/shard_map/relay/pallas_call | solution.py:566
  192.7 0.0 copy-start
  192.7 0.0 copy-start.1
  192.7 2.7 %copy.13 = bf16[1,6,32,4096]{3,2,1,0:T(8,128)(2,1)} copy(bf16[1,6,32,4096]{3,2,1,0:T(8,128)(2,1)} %bitcast.13) | data formatting | bytes 3145728
  195.4 0.0 copy-done
  195.4 0.6 copy.14
  196.1 0.0 copy-done.1
  196.1 0.6 copy.15
Async XLA Ops:
  192.7 2.7 %copy-start = (f32[64,128]{1,0:T(8,128)S(1)}, f32[64,128]{1,0:T(8,128)}, u32[]{:S(2)}) copy-start(f32[64,128]{1,0:T(8,128)} %get-tuple-element.7) | copy-start | bytes 98308
  192.7 3.3 %copy-start.1 = (f32[8,128]{1,0:T(8,128)S(1)}, f32[8,128]{1,0:T(8,128)}, u32[]{:S(2)}) copy-start(f32[8,128]{1,0:T(8,128)} %get-tuple-element.8) | copy-start | bytes 12292

commit v6 on v5

--- a/solution.py
+++ b/solution.py
@@ -346,7 +346,7 @@
         def _():
             pltpu.make_async_copy(gs.at[l, u], out.at[3 * yh + u], os.at[0, u]).start()
 
-        @pl.when(yh != l)
+        @pl.when((yh != l) & (u < 2))
         def _():
             send(gs.at[l, u], out.at[3 * yh + u], os.at[1, u], os.at[2, u], d_yo)
 
@@ -471,6 +471,12 @@
         s1[ym, hi_z, r, :] = (s1[ym, hi_z, r, :].astype(F32) + t2[:, r, :].astype(F32)).astype(BF16)
         send(s1.at[yp, :, r, :], v1.at[:, r, :], gsm.at[h, 6], gsm.at[h, 7], d_yp)
         send(s1.at[ym, :, r, :], v2.at[:, r, :], gsm.at[h, 8], gsm.at[h, 9], d_ym)
+    for l in range(2):
+
+        @pl.when(yh != l)
+        def _(l=l):
+            send(gs.at[l, 2], out.at[3 * yh + 2], os.at[1, 2], os.at[2, 2], d_yo)
+
     for h in range(2):
         r = rows_of(h)
         got(v1.at[:, r, :], gsm.at[h, 7])

time: 200 us -> 198 us (0.990)
  no operation moved by 1% of the time
where the time goes in v6:
time: 198 us; the launch traced here: 196 us
  Pallas kernels  192 us (97%)
  local copies, waits for them, and re-layouts  3.92 us (2%)
    pallas_call x1, Pallas kernels, run_all(): pl.pallas_call(functools.partial(kernel, dm), out_shape=(jax.ShapeDtypeSt...  192 us

profile of v6, /device:TPU:25, one launch (start us, length us, event | category | flops | bytes accessed | tf_op | source)
XLA Modules:
  0.0 196.4 jit_solution(1911059070225008860)
XLA Ops:
  0.6 191.9 %relay.1 = (bf16[6,32,4096]{2,1,0:T(8,128)(2,1)}, f32[64,128]{1,0:T(8,128)}, f32[8,128]{1,0:T(8,128)}) custom-call(s32[6]{0:T(128)} %order.1, bf16[64,512]{1,0:T(8,128)(2,1)} %bitcast.14, bf16[64,512]{1,0:T(8,128)(2,1)} %bitcast.15, bf16[64,128]{1,0:T(8,128)(2,1)} %bitcast.17, bf16[8,128]{1,0:T(8,128)(2,1)} %bitcast.19, bf16[6,32,4096]{2,1,0:T(8,128)(2,1)} %tok.1, ...), custom_call_target="tpu_custom_call" | custom-call | tf_op jit(solution)/shard_map/relay/pallas_call | solution.py:572
  192.5 0.0 copy-start
  192.5 0.0 copy-start.1
  192.5 2.7 %copy.13 = bf16[1,6,32,4096]{3,2,1,0:T(8,128)(2,1)} copy(bf16[1,6,32,4096]{3,2,1,0:T(8,128)(2,1)} %bitcast.13) | data formatting | bytes 3145728
  195.2 0.0 copy-done
  195.2 0.6 copy.14
  195.8 0.0 copy-done.1
  195.8 0.6 copy.15
Async XLA Ops:
  192.5 2.7 %copy-start = (f32[64,128]{1,0:T(8,128)S(1)}, f32[64,128]{1,0:T(8,128)}, u32[]{:S(2)}) copy-start(f32[64,128]{1,0:T(8,128)} %get-tuple-element.7) | copy-start | bytes 98308
  192.5 3.3 %copy-start.1 = (f32[8,128]{1,0:T(8,128)S(1)}, f32[8,128]{1,0:T(8,128)}, u32[]{:S(2)}) copy-start(f32[8,128]{1,0:T(8,128)} %get-tuple-element.8) | copy-start | bytes 12292

commit v7 on v6

--- a/solution.py
+++ b/solution.py
@@ -14,7 +14,8 @@
 NT = (((1,), (1,)), ((), ()))
 TN = (((0,), (0,)), ((), ()))
 NY = 4
-PIECES = 4
+PIECES = 8
+LANDING = 2
 
 
 def dot(a, b):
@@ -276,14 +277,15 @@
         for l in range(2):
             total = jnp.zeros((tokens, 128), F32)
             acc = jnp.zeros((tokens, hv + 128), F32)
-            for p in range(PIECES):
+            for p in range(0, PIECES, LANDING):
                 if l == 0:
 
                     @pl.when(x > 0)
                     def _(p=p):
-                        got(piece(xs, 0, u, p), fr.at[u, p])
-
-                for k in range(p * per_piece, (p + 1) * per_piece):
+                        for q in range(p, p + LANDING):
+                            got(piece(xs, 0, u, q), fr.at[u, q])
+
+                for k in range(p * per_piece, (p + LANDING) * per_piece):
                     v = xs[l, u, :, cols(k)]
                     acc = acc + dot(v, w_in(l, k))
                     v = v.astype(F32)
@@ -359,9 +361,10 @@
         @pl.when(x < nx - 1)
         def _():
             acc = jnp.zeros((tokens, hv), F32)
-            for p in range(PIECES):
-                got(piece(gs, 2, u, p), br.at[u, p])
-                for k in range(p * per_piece, (p + 1) * per_piece):
+            for p in range(0, PIECES, LANDING):
+                for q in range(p, p + LANDING):
+                    got(piece(gs, 2, u, q), br.at[u, q])
+                for k in range(p * per_piece, (p + LANDING) * per_piece):
                     acc = acc + dot(gs[2, u, :, cols(k)], w_back(1, k))
             both = adapter_side(1, u, acc)
             input_grad(1, u, both, lambda k: dot_nt(both, w_in(1, k)), lambda p: None)

time: 198 us -> 196 us (0.990)
  no operation moved by 1% of the time
where the time goes in v7:
time: 196 us
  Pallas kernels  191 us (97%)
  local copies, waits for them, and re-layouts  3.92 us (2%)
    pallas_call x1, Pallas kernels, run_all(): pl.pallas_call(functools.partial(kernel, dm), out_shape=(jax.ShapeDtypeSt...  191 us

profile of v7, /device:TPU:25, one launch (start us, length us, event | category | flops | bytes accessed | tf_op | source)
XLA Modules:
  0.0 196.0 jit_solution(4272482422134873972)
XLA Ops:
  0.6 191.4 %relay.1 = (bf16[6,32,4096]{2,1,0:T(8,128)(2,1)}, f32[64,128]{1,0:T(8,128)}, f32[8,128]{1,0:T(8,128)}) custom-call(s32[6]{0:T(128)} %order.1, bf16[64,512]{1,0:T(8,128)(2,1)} %bitcast.14, bf16[64,512]{1,0:T(8,128)(2,1)} %bitcast.15, bf16[64,128]{1,0:T(8,128)(2,1)} %bitcast.17, bf16[8,128]{1,0:T(8,128)(2,1)} %bitcast.19, bf16[6,32,4096]{2,1,0:T(8,128)(2,1)} %tok.1, ...), custom_call_target="tpu_custom_call" | custom-call | tf_op jit(solution)/shard_map/relay/pallas_call | solution.py:575
  192.0 0.0 copy-start
  192.1 0.0 copy-start.1
  192.1 2.7 %copy.13 = bf16[1,6,32,4096]{3,2,1,0:T(8,128)(2,1)} copy(bf16[1,6,32,4096]{3,2,1,0:T(8,128)(2,1)} %bitcast.13) | data formatting | bytes 3145728
  194.8 0.0 copy-done
  194.8 0.6 copy.14
  195.4 0.0 copy-done.1
  195.4 0.6 copy.15
Async XLA Ops:
  192.0 2.7 %copy-start = (f32[64,128]{1,0:T(8,128)S(1)}, f32[64,128]{1,0:T(8,128)}, u32[]{:S(2)}) copy-start(f32[64,128]{1,0:T(8,128)} %get-tuple-element.7) | copy-start | bytes 98308
  192.1 3.3 %copy-start.1 = (f32[8,128]{1,0:T(8,128)S(1)}, f32[8,128]{1,0:T(8,128)}, u32[]{:S(2)}) copy-start(f32[8,128]{1,0:T(8,128)} %get-tuple-element.8) | copy-start | bytes 12292
